TPU v7x, 32 devices: a whole 2x2x4 slice. The times are simulated.
32 devices in a mesh: section: 8 (over y, x, core), tp: 4 (over z).
Axes of the slice: x: 2, y: 2, z: 4, core: 2. Of those that a mesh axis runs over, the one named last changes fastest.
Arguments:
- tokens: bfloat16 [512, 2048], P('tp'), may hold values from -6 to 6
- cotangent: bfloat16 [512, 2048], P('tp'), may hold values from -0.119628906 to 0.119628906
- value_weight: bfloat16 [8, 2048, 512], P('section', None, 'tp'), may hold values from -0.125 to 0.125
- output_weight: bfloat16 [8, 2048, 512], P('section', None, 'tp'), may hold values from -0.25 to 0.25
- value_first: float32 [8, 2048, 512], P('section', None, 'tp'), may hold values from -1.8 to 1.8
- output_first: float32 [8, 2048, 512], P('section', None, 'tp'), may hold values from -1.8 to 1.8
- value_second: float32 [8, 2048, 512], P('section', None, 'tp'), may hold values from 0.01 to 1
- output_second: float32 [8, 2048, 512], P('section', None, 'tp'), may hold values from 0.01 to 1
- layer_map: int32 [6], replicated, may hold values from 0 to 3, as said below
- old_section: int32 [4], replicated, may hold values from 0 to 7, as said below
- new_section: int32 [6], replicated, may hold values from 0 to 7, as said below
Outputs:
- new_value_weight: bfloat16 [8, 2048, 512], P('section', None, 'tp')
- new_output_weight: bfloat16 [8, 2048, 512], P('section', None, 'tp')
- new_value_first: float32 [8, 2048, 512], P('section', None, 'tp')
- new_output_first: float32 [8, 2048, 512], P('section', None, 'tp')
- new_value_second: float32 [8, 2048, 512], P('section', None, 'tp')
- new_output_second: float32 [8, 2048, 512], P('section', None, 'tp')
Inputs may be any that keep to these rules, and one draw needn't show every extreme that they name: `layer_map`: Non-decreasing; every old layer appears once or twice. `old_section`: strictly increasing. `new_section`: strictly increasing.
All inputs are finite; a program needn't handle non-finite values.
Results may differ from a plain program's by a relative error of at most 0.025.
Values may be sent and summed in bfloat16 or wider, within the bound.
No kernel may reach another device: no remote copies, remote signals or barrier semaphores. Data moves between devices by JAX's collectives and lax.ppermute only.
A program may use at most 128 MiB of HBM per device.

v0:
```python
import jax
import jax.numpy as jnp
from jax import lax
from jax.sharding import PartitionSpec as P

epsilon = 1e-05
beta_one = 0.9
beta_two = 0.95
step_rate = 0.003
adam_floor = 1e-08


def passed_along(block, axis, distance):
    devices = range(lax.axis_size(axis))
    route = [(i - distance, i) for i in devices if i - distance in devices]
    return lax.ppermute(block, axis, route)


def normalize(stream):
    widened = stream.astype(jnp.float32)
    factor = lax.rsqrt(jnp.mean(widened * widened, axis=-1, keepdims=True) + epsilon)
    return (widened * factor, factor)


def forward_layer(stream, value_full, output_full):
    normed, factor = normalize(stream)
    hidden = normed.astype(jnp.bfloat16)
    preact = jnp.dot(hidden, value_full, preferred_element_type=jnp.float32)
    unit_values = jax.nn.silu(preact).astype(jnp.bfloat16)
    mixing = lax.dot_general(
        unit_values, output_full, (((1,), (1,)), ((), ())), preferred_element_type=jnp.float32
    )
    return ((stream.astype(jnp.float32) + mixing).astype(jnp.bfloat16), preact, unit_values)


def backward_layer(stream, preact, grad_out, value_full, output_full):
    grad_units = jnp.dot(grad_out, output_full, preferred_element_type=jnp.float32)
    gate_value = jax.nn.sigmoid(preact)
    grad_inner = (grad_units * gate_value * (1.0 + preact * (1.0 - gate_value))).astype(
        jnp.bfloat16
    )
    grad_hidden = lax.dot_general(
        grad_inner, value_full, (((1,), (1,)), ((), ())), preferred_element_type=jnp.float32
    )
    normed, factor = normalize(stream)
    grad_stream = factor * (
        grad_hidden - normed * jnp.mean(grad_hidden * normed, axis=-1, keepdims=True)
    )
    return ((grad_out.astype(jnp.float32) + grad_stream).astype(jnp.bfloat16), grad_inner)


def hand_over(values, offset):
    return passed_along(values, "section", offset)


def adam_update(weight, first, second, gradient):
    first_new = beta_one * first + (1.0 - beta_one) * gradient
    second_new = beta_two * second + (1.0 - beta_two) * gradient * gradient
    weight_new = (
        weight.astype(jnp.float32) - step_rate * first_new / (jnp.sqrt(second_new) + adam_floor)
    ).astype(jnp.bfloat16)
    return (weight_new[None], first_new[None], second_new[None])


def body(
    tokens,
    cotangent,
    value_weight,
    output_weight,
    value_first,
    output_first,
    value_second,
    output_second,
    layer_map,
    old_section,
    new_section,
):
    sections = lax.axis_size("section")
    myself = lax.axis_index("section")
    positions = lax.iota(jnp.int32, sections)
    owner_match = new_section[None, :] == positions[:, None]
    has_layer = jnp.any(owner_match, axis=1)
    new_index = jnp.sum(
        jnp.where(owner_match, lax.iota(jnp.int32, new_section.shape[0])[None, :], 0), axis=1
    )
    map_match = new_index[:, None] == lax.iota(jnp.int32, layer_map.shape[0])[None, :]
    old_index = jnp.sum(jnp.where(map_match, layer_map[None, :], 0), axis=1)
    section_match = old_index[:, None] == lax.iota(jnp.int32, old_section.shape[0])[None, :]
    source = jnp.sum(jnp.where(section_match, old_section[None, :], 0), axis=1)
    holds_layer = jnp.any((positions == myself) & has_layer)
    keep_mask = has_layer.astype(jnp.float32)[:, None, None]
    spread_pieces = (
        lax.all_to_all(
            value_weight.astype(jnp.float32), "section", split_axis=1, concat_axis=0, tiled=True
        ),
        lax.all_to_all(
            output_weight.astype(jnp.float32), "section", split_axis=1, concat_axis=0, tiled=True
        ),
        lax.all_to_all(value_first, "section", split_axis=1, concat_axis=0, tiled=True),
        lax.all_to_all(output_first, "section", split_axis=1, concat_axis=0, tiled=True),
        lax.all_to_all(value_second, "section", split_axis=1, concat_axis=0, tiled=True),
        lax.all_to_all(output_second, "section", split_axis=1, concat_axis=0, tiled=True),
    )
    chosen = [jnp.take(portion, source, axis=0) * keep_mask for portion in spread_pieces]
    arrived = (
        lax.all_to_all(chosen[0], "section", split_axis=0, concat_axis=1, tiled=True),
        lax.all_to_all(chosen[1], "section", split_axis=0, concat_axis=1, tiled=True),
        lax.all_to_all(chosen[2], "section", split_axis=0, concat_axis=1, tiled=True),
        lax.all_to_all(chosen[3], "section", split_axis=0, concat_axis=1, tiled=True),
        lax.all_to_all(chosen[4], "section", split_axis=0, concat_axis=1, tiled=True),
        lax.all_to_all(chosen[5], "section", split_axis=0, concat_axis=1, tiled=True),
    )
    value_local = arrived[0][0].astype(jnp.bfloat16)
    output_local = arrived[1][0].astype(jnp.bfloat16)
    first_value = arrived[2][0]
    first_output = arrived[3][0]
    second_value = arrived[4][0]
    second_output = arrived[5][0]
    value_full, output_full = (
        lax.all_gather(value_local, "tp", axis=1, tiled=True),
        lax.all_gather(output_local, "tp", axis=1, tiled=True),
    )
    row_count, feature_count = tokens.shape
    channel_count = value_full.shape[1]
    blocks = 1
    block_rows = row_count // blocks
    step_count = sections + blocks - 1
    token_blocks = tokens.reshape(blocks, block_rows, feature_count)
    grad_blocks = cotangent.reshape(blocks, block_rows, feature_count)

    def forward_step(step_index, loop_state):
        stream, saved_in, saved_pre, saved_units = loop_state
        entering = token_blocks[jnp.minimum(step_index, blocks - 1)]
        stream = jnp.where(myself == 0, entering, stream)
        block_slot = step_index - myself
        active = (block_slot >= 0) & (block_slot < blocks)
        block_place = jnp.clip(block_slot, 0, blocks - 1)
        result, preact, unit_values = forward_layer(stream, value_full, output_full)
        result = jnp.where(holds_layer, result, stream)
        saved_in = jnp.where(
            active, lax.dynamic_update_index_in_dim(saved_in, stream, block_place, 0), saved_in
        )
        saved_pre = jnp.where(
            active, lax.dynamic_update_index_in_dim(saved_pre, preact, block_place, 0), saved_pre
        )
        saved_units = jnp.where(
            active,
            lax.dynamic_update_index_in_dim(saved_units, unit_values, block_place, 0),
            saved_units,
        )
        return (hand_over(result, 1), saved_in, saved_pre, saved_units)

    forward_init = (
        token_blocks[0],
        jnp.zeros((blocks, block_rows, feature_count), jnp.bfloat16),
        jnp.zeros((blocks, block_rows, channel_count), jnp.float32),
        jnp.zeros((blocks, block_rows, channel_count), jnp.bfloat16),
    )
    stream_last, saved_in, saved_pre, saved_units = lax.fori_loop(
        0, step_count, forward_step, forward_init
    )

    def backward_step(step_index, loop_state):
        flowing, saved_grad, saved_inner = loop_state
        entering = grad_blocks[jnp.minimum(step_index, blocks - 1)]
        flowing = jnp.where(myself == sections - 1, entering, flowing)
        block_slot = step_index - (sections - 1 - myself)
        active = (block_slot >= 0) & (block_slot < blocks)
        block_place = jnp.clip(block_slot, 0, blocks - 1)
        stream_in = saved_in[block_place]
        preact = saved_pre[block_place]
        result, grad_inner = backward_layer(stream_in, preact, flowing, value_full, output_full)
        result = jnp.where(holds_layer, result, flowing)
        saved_grad = jnp.where(
            active, lax.dynamic_update_index_in_dim(saved_grad, flowing, block_place, 0), saved_grad
        )
        saved_inner = jnp.where(
            active,
            lax.dynamic_update_index_in_dim(saved_inner, grad_inner, block_place, 0),
            saved_inner,
        )
        return (hand_over(result, -1), saved_grad, saved_inner)

    backward_init = (
        grad_blocks[0],
        jnp.zeros((blocks, block_rows, feature_count), jnp.bfloat16),
        jnp.zeros((blocks, block_rows, channel_count), jnp.bfloat16),
    )
    flowing_last, saved_grad, saved_inner = lax.fori_loop(
        0, step_count, backward_step, backward_init
    )
    hidden_all = normalize(saved_in.reshape(row_count, feature_count))[0].astype(jnp.bfloat16)
    grad_value = lax.dot_general(
        hidden_all,
        saved_inner.reshape(row_count, channel_count),
        (((0,), (0,)), ((), ())),
        preferred_element_type=jnp.float32,
    )
    grad_output = lax.dot_general(
        saved_grad.reshape(row_count, feature_count),
        saved_units.reshape(row_count, channel_count),
        (((0,), (0,)), ((), ())),
        preferred_element_type=jnp.float32,
    )
    grad_value, grad_output = (
        lax.psum_scatter(
            grad_value.astype(jnp.bfloat16), "tp", scatter_dimension=1, tiled=True
        ).astype(jnp.float32),
        lax.psum_scatter(
            grad_output.astype(jnp.bfloat16), "tp", scatter_dimension=1, tiled=True
        ).astype(jnp.float32),
    )
    owned = holds_layer.astype(jnp.float32)
    grad_value = grad_value * owned
    grad_output = grad_output * owned
    value_new = adam_update(value_local, first_value, second_value, grad_value)
    output_new = adam_update(output_local, first_output, second_output, grad_output)
    return (value_new[0], output_new[0], value_new[1], output_new[1], value_new[2], output_new[2])


def solution(mesh):
    placed = (
        P("tp", None),
        P("tp", None),
        P("section", None, "tp"),
        P("section", None, "tp"),
        P("section", None, "tp"),
        P("section", None, "tp"),
        P("section", None, "tp"),
        P("section", None, "tp"),
        P(),
        P(),
        P(),
    )
    return jax.shard_map(
        body,
        mesh=mesh,
        in_specs=placed,
        out_specs=(
            P("section", None, "tp"),
            P("section", None, "tp"),
            P("section", None, "tp"),
            P("section", None, "tp"),
            P("section", None, "tp"),
            P("section", None, "tp"),
        ),
        check_vma=False,
    )
```

profile of v0, /device:TPU:19, one launch (start us, length us, event | category | flops | bytes accessed | tf_op | source)
XLA Modules:
  0.0 585.9 jit_solution(15786482571888250535)
XLA Ops:
  9.3 4.5 all-to-all-start
  14.9 12.8 %all-to-all-done = f32[1,2048,128]{2,0,1:T(1,128)S(1)} async-done(((f32[1,2048,128]{2,0,1:T(1,128)}), f32[1,2048,128]{2,0,1:T(1,128)S(1)}, u32[]{:S(2)}, u32[]{:S(2)}) %all-to-all-start) | async-done | bytes 1048608 | tf_op jit(solution)/shard_map/all_to_all | solution.py:93
  27.7 5.0 all-to-all-start.4
  34.5 12.0 %all-to-all-done.4 = f32[1,2048,128]{2,0,1:T(1,128)S(1)} async-done(((f32[1,2048,128]{2,0,1:T(1,128)}), f32[1,2048,128]{2,0,1:T(1,128)S(1)}, u32[]{:S(2)}, u32[]{:S(2)}) %all-to-all-start.4) | async-done | bytes 1048608 | tf_op jit(solution)/shard_map/all_to_all | solution.py:96
  47.5 12.7 %all_to_all.126 = bf16[8,256,128]{2,1,0:T(8,128)(2,1)} all-to-all(bf16[8,256,128]{2,1,0:T(8,128)(2,1)S(1)} %get-tuple-element.642), channel_id=1, replica_groups=mesh['section'=8,'tp'=4] {'section'}, dimensions={0} | all-to-all | bytes 1048576 | tf_op jit(solution)/shard_map/all_to_all | solution.py:106
  60.3 12.8 %all_to_all.127 = bf16[8,256,128]{2,1,0:T(8,128)(2,1)} all-to-all(bf16[8,256,128]{2,1,0:T(8,128)(2,1)S(1)} %get-tuple-element.641), channel_id=1, replica_groups=mesh['section'=8,'tp'=4] {'section'}, dimensions={0} | all-to-all | bytes 1048576 | tf_op jit(solution)/shard_map/all_to_all | solution.py:107
  73.1 6.0 %all-to-all-start.8 = ((f32[1,2048,128]{2,0,1:T(1,128)}), f32[1,2048,128]{2,0,1:T(1,128)}, u32[]{:S(2)}, u32[]{:S(2)}) async-start(f32[1,2048,128]{2,0,1:T(1,128)} %bitcast.128), calls=%async_computation.8 | async-start | bytes 2097152 | tf_op jit(solution)/shard_map/all_to_all | solution.py:100
  79.9 24.8 %all-gather.3.cloned.1.call-done = bf16[2048,512]{1,0:T(8,128)(2,1)} async-done(((bf16[2048,128]{1,0:T(8,128)(2,1)}), bf16[2048,512]{1,0:T(8,128)(2,1)}) %all-gather.3.cloned.1.call-update) | async-done | bytes 2097168 | tf_op jit(solution)/shard_map/all_gather | solution.py:120
  104.7 46.0 %all-gather.5.cloned.1.call-done = bf16[2048,512]{1,0:T(8,128)(2,1)} async-done(((bf16[2048,128]{1,0:T(8,128)(2,1)}), bf16[2048,512]{1,0:T(8,128)(2,1)}) %all-gather.5.cloned.1.call-update) | async-done | bytes 2097168 | tf_op jit(solution)/shard_map/all_gather | solution.py:121
  150.7 126.6 %while.41 = (s32[]{:T(128)}, bf16[128,2048]{1,0:T(8,128)(2,1)S(1)}, bf16[1,128,2048]{2,1,0:T(8,128)(2,1)S(1)}, f32[1,128,512]{2,1,0:T(8,128)}, bf16[1,128,512]{2...) while((s32[]{:T(128)}, bf16[128,2048]{1,0:T(8,128)(2,1)S(1)}, ...), condition=%wide.region_7.9_spmd.clone, body=%wide.region_5.8_spmd.clone.sunk | while | flops 541196416 | bytes 31459656 | solution.py:159
  155.4 3.8 collective-permute-start
  159.3 6.0 %collective-permute-done = bf16[128,2048]{1,0:T(8,128)(2,1)S(1)} collective-permute-done((bf16[128,2048]{1,0:T(8,128)(2,1)S(1)}, bf16[128,2048]{1,0:T(8,128)(2,1)S(1)}, u32[]{:S(2)}, u32[]{:S(2)}) %collective-permute-start) | collective-permute-done | bytes 524320 | tf_op jit(solution)/shard_map/while/body/eval_jaxpr/ppermute | solution.py:16
  169.9 5.3 collective-permute-start
  175.3 6.0 %collective-permute-done = bf16[128,2048]{1,0:T(8,128)(2,1)S(1)} collective-permute-done((bf16[128,2048]{1,0:T(8,128)(2,1)S(1)}, bf16[128,2048]{1,0:T(8,128)(2,1)S(1)}, u32[]{:S(2)}, u32[]{:S(2)}) %collective-permute-start) | collective-permute-done | bytes 524320 | tf_op jit(solution)/shard_map/while/body/eval_jaxpr/ppermute | solution.py:16
  185.9 5.3 collective-permute-start
  191.3 6.0 %collective-permute-done = bf16[128,2048]{1,0:T(8,128)(2,1)S(1)} collective-permute-done((bf16[128,2048]{1,0:T(8,128)(2,1)S(1)}, bf16[128,2048]{1,0:T(8,128)(2,1)S(1)}, u32[]{:S(2)}, u32[]{:S(2)}) %collective-permute-start) | collective-permute-done | bytes 524320 | tf_op jit(solution)/shard_map/while/body/eval_jaxpr/ppermute | solution.py:16
  201.9 5.3 collective-permute-start
  207.3 6.0 %collective-permute-done = bf16[128,2048]{1,0:T(8,128)(2,1)S(1)} collective-permute-done((bf16[128,2048]{1,0:T(8,128)(2,1)S(1)}, bf16[128,2048]{1,0:T(8,128)(2,1)S(1)}, u32[]{:S(2)}, u32[]{:S(2)}) %collective-permute-start) | collective-permute-done | bytes 524320 | tf_op jit(solution)/shard_map/while/body/eval_jaxpr/ppermute | solution.py:16
  217.9 5.3 collective-permute-start
  223.3 6.0 %collective-permute-done = bf16[128,2048]{1,0:T(8,128)(2,1)S(1)} collective-permute-done((bf16[128,2048]{1,0:T(8,128)(2,1)S(1)}, bf16[128,2048]{1,0:T(8,128)(2,1)S(1)}, u32[]{:S(2)}, u32[]{:S(2)}) %collective-permute-start) | collective-permute-done | bytes 524320 | tf_op jit(solution)/shard_map/while/body/eval_jaxpr/ppermute | solution.py:16
  233.9 5.3 collective-permute-start
  239.3 6.0 %collective-permute-done = bf16[128,2048]{1,0:T(8,128)(2,1)S(1)} collective-permute-done((bf16[128,2048]{1,0:T(8,128)(2,1)S(1)}, bf16[128,2048]{1,0:T(8,128)(2,1)S(1)}, u32[]{:S(2)}, u32[]{:S(2)}) %collective-permute-start) | collective-permute-done | bytes 524320 | tf_op jit(solution)/shard_map/while/body/eval_jaxpr/ppermute | solution.py:16
  249.9 5.3 collective-permute-start
  255.3 6.0 %collective-permute-done = bf16[128,2048]{1,0:T(8,128)(2,1)S(1)} collective-permute-done((bf16[128,2048]{1,0:T(8,128)(2,1)S(1)}, bf16[128,2048]{1,0:T(8,128)(2,1)S(1)}, u32[]{:S(2)}, u32[]{:S(2)}) %collective-permute-start) | collective-permute-done | bytes 524320 | tf_op jit(solution)/shard_map/while/body/eval_jaxpr/ppermute | solution.py:16
  265.9 5.3 collective-permute-start
  271.3 6.0 %collective-permute-done = bf16[128,2048]{1,0:T(8,128)(2,1)S(1)} collective-permute-done((bf16[128,2048]{1,0:T(8,128)(2,1)S(1)}, bf16[128,2048]{1,0:T(8,128)(2,1)S(1)}, u32[]{:S(2)}, u32[]{:S(2)}) %collective-permute-start) | collective-permute-done | bytes 524320 | tf_op jit(solution)/shard_map/while/body/eval_jaxpr/ppermute | solution.py:16
  278.3 148.2 %while.42 = (s32[]{:T(128)}, bf16[128,2048]{1,0:T(8,128)(2,1)}, bf16[1,128,2048]{2,1,0:T(8,128)(2,1)}, bf16[1,128,512]{2,1,0:T(8,128)(2,1)}, pred[]{:T(512)}, /*...) while((s32[]{:T(128)}, bf16[128,2048]{1,0:T(8,128)(2,1)}, ...), condition=%wide.region_12.14_spmd.clone, body=%wide.region_9.13_spmd.clone.sunk | while | flops 542507136 | bytes 36180876 | solution.py:189
  286.4 10.2 %collective-permute-done.1 = bf16[128,2048]{1,0:T(8,128)(2,1)S(1)} collective-permute-done((bf16[128,2048]{1,0:T(8,128)(2,1)S(1)}, bf16[128,2048]{1,0:T(8,128)(2,1)S(1)}, u32[]{:S(2)}, u32[]{:S(2)}) %collective-permute-start.1) | collective-permute-done | bytes 524320 | tf_op jit(solution)/shard_map/while/body/eval_jaxpr/ppermute | solution.py:16
  305.6 9.5 %collective-permute-done.1 = bf16[128,2048]{1,0:T(8,128)(2,1)S(1)} collective-permute-done((bf16[128,2048]{1,0:T(8,128)(2,1)S(1)}, bf16[128,2048]{1,0:T(8,128)(2,1)S(1)}, u32[]{:S(2)}, u32[]{:S(2)}) %collective-permute-start.1) | collective-permute-done | bytes 524320 | tf_op jit(solution)/shard_map/while/body/eval_jaxpr/ppermute | solution.py:16
  324.0 9.5 %collective-permute-done.1 = bf16[128,2048]{1,0:T(8,128)(2,1)S(1)} collective-permute-done((bf16[128,2048]{1,0:T(8,128)(2,1)S(1)}, bf16[128,2048]{1,0:T(8,128)(2,1)S(1)}, u32[]{:S(2)}, u32[]{:S(2)}) %collective-permute-start.1) | collective-permute-done | bytes 524320 | tf_op jit(solution)/shard_map/while/body/eval_jaxpr/ppermute | solution.py:16
  342.5 9.5 %collective-permute-done.1 = bf16[128,2048]{1,0:T(8,128)(2,1)S(1)} collective-permute-done((bf16[128,2048]{1,0:T(8,128)(2,1)S(1)}, bf16[128,2048]{1,0:T(8,128)(2,1)S(1)}, u32[]{:S(2)}, u32[]{:S(2)}) %collective-permute-start.1) | collective-permute-done | bytes 524320 | tf_op jit(solution)/shard_map/while/body/eval_jaxpr/ppermute | solution.py:16
  360.9 9.5 %collective-permute-done.1 = bf16[128,2048]{1,0:T(8,128)(2,1)S(1)} collective-permute-done((bf16[128,2048]{1,0:T(8,128)(2,1)S(1)}, bf16[128,2048]{1,0:T(8,128)(2,1)S(1)}, u32[]{:S(2)}, u32[]{:S(2)}) %collective-permute-start.1) | collective-permute-done | bytes 524320 | tf_op jit(solution)/shard_map/while/body/eval_jaxpr/ppermute | solution.py:16
  379.4 9.5 %collective-permute-done.1 = bf16[128,2048]{1,0:T(8,128)(2,1)S(1)} collective-permute-done((bf16[128,2048]{1,0:T(8,128)(2,1)S(1)}, bf16[128,2048]{1,0:T(8,128)(2,1)S(1)}, u32[]{:S(2)}, u32[]{:S(2)}) %collective-permute-start.1) | collective-permute-done | bytes 524320 | tf_op jit(solution)/shard_map/while/body/eval_jaxpr/ppermute | solution.py:16
  397.8 9.5 %collective-permute-done.1 = bf16[128,2048]{1,0:T(8,128)(2,1)S(1)} collective-permute-done((bf16[128,2048]{1,0:T(8,128)(2,1)S(1)}, bf16[128,2048]{1,0:T(8,128)(2,1)S(1)}, u32[]{:S(2)}, u32[]{:S(2)}) %collective-permute-start.1) | collective-permute-done | bytes 524320 | tf_op jit(solution)/shard_map/while/body/eval_jaxpr/ppermute | solution.py:16
  416.3 9.5 %collective-permute-done.1 = bf16[128,2048]{1,0:T(8,128)(2,1)S(1)} collective-permute-done((bf16[128,2048]{1,0:T(8,128)(2,1)S(1)}, bf16[128,2048]{1,0:T(8,128)(2,1)S(1)}, u32[]{:S(2)}, u32[]{:S(2)}) %collective-permute-start.1) | collective-permute-done | bytes 524320 | tf_op jit(solution)/shard_map/while/body/eval_jaxpr/ppermute | solution.py:16
  432.0 16.6 %all_to_all.128 = f32[1,2048,128]{2,0,1:T(1,128)} all-to-all(f32[1,2048,128]{2,0,1:T(1,128)S(1)} %bitcast.129), channel_id=1, replica_groups=mesh['section'=8,'tp'=4] {'section'}, dimensions={1} | all-to-all | bytes 2097152 | tf_op jit(solution)/shard_map/all_to_all | solution.py:102
  448.5 18.9 %all_to_all.129 = f32[1,2048,128]{2,0,1:T(1,128)S(1)} all-to-all(f32[1,2048,128]{2,0,1:T(1,128)} %bitcast.130), channel_id=1, replica_groups=mesh['section'=8,'tp'=4] {'section'}, dimensions={1} | all-to-all | bytes 2097152 | tf_op jit(solution)/shard_map/all_to_all | solution.py:99
  467.4 5.1 all-to-all-start.6
  472.5 2.8 gather_fusion.4
  475.3 2.8 gather_fusion.5
  479.7 6.6 %all-to-all-done.6 = f32[1,2048,128]{2,0,1:T(1,128)S(1)} async-done(((f32[1,2048,128]{2,0,1:T(1,128)}), f32[1,2048,128]{2,0,1:T(1,128)S(1)}, u32[]{:S(2)}, u32[]{:S(2)}) %all-to-all-start.6) | async-done | bytes 1048608 | tf_op jit(solution)/shard_map/all_to_all | solution.py:101
  492.9 3.0 select_multiply_fusion
  495.9 17.7 %all_to_all.130 = f32[8,256,128]{2,1,0:T(8,128)S(1)} all-to-all(f32[8,256,128]{2,1,0:T(8,128)S(1)} %get-tuple-element.637), channel_id=1, replica_groups=mesh['section'=8,'tp'=4] {'section'}, dimensions={0} | all-to-all | bytes 2097152 | tf_op jit(solution)/shard_map/all_to_all | solution.py:111
  513.6 18.3 %all_to_all.131 = f32[8,256,128]{2,1,0:T(8,128)} all-to-all(f32[8,256,128]{2,1,0:T(8,128)S(1)} %get-tuple-element.640), channel_id=1, replica_groups=mesh['section'=8,'tp'=4] {'section'}, dimensions={0} | all-to-all | bytes 2097152 | tf_op jit(solution)/shard_map/all_to_all | solution.py:109
  531.9 18.4 %all_to_all.132 = f32[8,256,128]{2,1,0:T(8,128)} all-to-all(f32[8,256,128]{2,1,0:T(8,128)S(1)} %get-tuple-element.639), channel_id=1, replica_groups=mesh['section'=8,'tp'=4] {'section'}, dimensions={0} | all-to-all | bytes 2097152 | tf_op jit(solution)/shard_map/all_to_all | solution.py:110
  550.4 5.2 all-to-all-start.3
  559.7 9.7 %all-to-all-done.3 = f32[8,256,128]{2,1,0:T(8,128)S(1)} async-done(((f32[8,256,128]{2,1,0:T(8,128)}), f32[8,256,128]{2,1,0:T(8,128)S(1)}, u32[]{:S(2)}, u32[]{:S(2)}) %all-to-all-start.3) | async-done | bytes 1048608 | tf_op jit(solution)/shard_map/all_to_all | solution.py:108
  573.9 3.4 fusion.28
  (347 shorter events, 139.8 us)
Async XLA Ops:
  7.2 6.7 %copy-start.16 = (bf16[1,2048,128]{2,1,0:T(8,128)(2,1)S(1)}, bf16[1,2048,128]{2,1,0:T(8,128)(2,1)}, u32[]{:S(2)}) copy-start(bf16[1,2048,128]{2,1,0:T(8,128)(2,1)} %param.20) | copy-start | bytes 1572868
  9.3 18.4 %all-to-all-start = ((f32[1,2048,128]{2,0,1:T(1,128)}), f32[1,2048,128]{2,0,1:T(1,128)S(1)}, u32[]{:S(2)}, u32[]{:S(2)}) async-start(f32[1,2048,128]{2,0,1:T(1,128)} %bitcast), calls=%async_computation | async-start | bytes 2097152 | tf_op jit(solution)/shard_map/all_to_all | solution.py:93
  13.9 18.9 %copy-start.22 = (s32[6]{0:T(128)S(1)}, s32[6]{0:T(128)}, u32[]{:S(2)}) copy-start(s32[6]{0:T(128)} %param.27) | copy-start | bytes 76
  13.9 19.1 %copy-start.23 = (s32[6]{0:T(128)S(1)}, s32[6]{0:T(128)}, u32[]{:S(2)}) copy-start(s32[6]{0:T(128)} %param.25) | copy-start | bytes 76
  13.9 19.3 %copy-start.24 = (s32[4]{0:T(128)S(1)}, s32[4]{0:T(128)}, u32[]{:S(2)}) copy-start(s32[4]{0:T(128)} %param.26) | copy-start | bytes 52
  27.7 18.9 %all-to-all-start.4 = ((f32[1,2048,128]{2,0,1:T(1,128)}), f32[1,2048,128]{2,0,1:T(1,128)S(1)}, u32[]{:S(2)}, u32[]{:S(2)}) async-start(f32[1,2048,128]{2,0,1:T(1,128)} %bitcast.7), calls=%async_computation.4 | async-start | bytes 2097152 | tf_op jit(solution)/shard_map/all_to_all | solution.py:96
  32.7 72.0 %all-gather.3.cloned.1.call-start = ((), (), s32[]{:S(2)}) async-start(), calls=%async_computation.14 | async-start | bytes 2621440 | tf_op jit(solution)/shard_map/all_gather | solution.py:120
  60.2 90.5 %all-gather.5.cloned.1.call-start = ((), (), s32[]{:S(2)}) async-start(), calls=%async_computation.15 | async-start | bytes 2621440 | tf_op jit(solution)/shard_map/all_gather | solution.py:121
  73.1 6.1 %copy-start.3 = (bf16[128,2048]{1,0:T(8,128)(2,1)S(1)}, bf16[128,2048]{1,0:T(8,128)(2,1)}, u32[]{:S(2)}) copy-start(bf16[128,2048]{1,0:T(8,128)(2,1)} %param.18) | copy-start | bytes 1572868
  73.1 77.6 %copy-start.2 = (bf16[128,2048]{1,0:T(8,128)(2,1)S(1)}, bf16[128,2048]{1,0:T(8,128)(2,1)}, u32[]{:S(2)}) copy-start(bf16[128,2048]{1,0:T(8,128)(2,1)} %param.17) | copy-start | bytes 1572868
  73.1 357.7 %all-to-all-start.8 = ((f32[1,2048,128]{2,0,1:T(1,128)}), f32[1,2048,128]{2,0,1:T(1,128)}, u32[]{:S(2)}, u32[]{:S(2)}) async-start(f32[1,2048,128]{2,0,1:T(1,128)} %bitcast.128), calls=%async_computation.8 | async-start | bytes 2097152 | tf_op jit(solution)/shard_map/all_to_all | solution.py:100
  79.1 491.4 %reduce-scatter.9.cloned.1.call-start = ((), (), s32[]{:S(2)}) async-start(), calls=%async_computation.17 | async-start | bytes 2621440
  155.4 9.9 %collective-permute-start = (bf16[128,2048]{1,0:T(8,128)(2,1)S(1)}, bf16[128,2048]{1,0:T(8,128)(2,1)S(1)}, u32[]{:S(2)}, u32[]{:S(2)}) collective-permute-start(bf16[128,2048]{1,0:T(8,128)(2,1)S(1)} %fusion.54), channel_id=1, source_target_pairs={{0,4},{4,8},{8,12},{12,16},{16,20},{20,24},{24,28},{1,5},{5,9},{9,... | collective-permute-start | bytes 1572872 | tf_op jit(solution)/shard_map/while/body/eval_jaxpr/ppermute | solution.py:16
  169.9 11.4 %collective-permute-start = (bf16[128,2048]{1,0:T(8,128)(2,1)S(1)}, bf16[128,2048]{1,0:T(8,128)(2,1)S(1)}, u32[]{:S(2)}, u32[]{:S(2)}) collective-permute-start(bf16[128,2048]{1,0:T(8,128)(2,1)S(1)} %fusion.54), channel_id=1, source_target_pairs={{0,4},{4,8},{8,12},{12,16},{16,20},{20,24},{24,28},{1,5},{5,9},{9,... | collective-permute-start | bytes 1572872 | tf_op jit(solution)/shard_map/while/body/eval_jaxpr/ppermute | solution.py:16
  185.9 11.4 %collective-permute-start = (bf16[128,2048]{1,0:T(8,128)(2,1)S(1)}, bf16[128,2048]{1,0:T(8,128)(2,1)S(1)}, u32[]{:S(2)}, u32[]{:S(2)}) collective-permute-start(bf16[128,2048]{1,0:T(8,128)(2,1)S(1)} %fusion.54), channel_id=1, source_target_pairs={{0,4},{4,8},{8,12},{12,16},{16,20},{20,24},{24,28},{1,5},{5,9},{9,... | collective-permute-start | bytes 1572872 | tf_op jit(solution)/shard_map/while/body/eval_jaxpr/ppermute | solution.py:16
  201.9 11.4 %collective-permute-start = (bf16[128,2048]{1,0:T(8,128)(2,1)S(1)}, bf16[128,2048]{1,0:T(8,128)(2,1)S(1)}, u32[]{:S(2)}, u32[]{:S(2)}) collective-permute-start(bf16[128,2048]{1,0:T(8,128)(2,1)S(1)} %fusion.54), channel_id=1, source_target_pairs={{0,4},{4,8},{8,12},{12,16},{16,20},{20,24},{24,28},{1,5},{5,9},{9,... | collective-permute-start | bytes 1572872 | tf_op jit(solution)/shard_map/while/body/eval_jaxpr/ppermute | solution.py:16
  217.9 11.4 %collective-permute-start = (bf16[128,2048]{1,0:T(8,128)(2,1)S(1)}, bf16[128,2048]{1,0:T(8,128)(2,1)S(1)}, u32[]{:S(2)}, u32[]{:S(2)}) collective-permute-start(bf16[128,2048]{1,0:T(8,128)(2,1)S(1)} %fusion.54), channel_id=1, source_target_pairs={{0,4},{4,8},{8,12},{12,16},{16,20},{20,24},{24,28},{1,5},{5,9},{9,... | collective-permute-start | bytes 1572872 | tf_op jit(solution)/shard_map/while/body/eval_jaxpr/ppermute | solution.py:16
  233.9 11.4 %collective-permute-start = (bf16[128,2048]{1,0:T(8,128)(2,1)S(1)}, bf16[128,2048]{1,0:T(8,128)(2,1)S(1)}, u32[]{:S(2)}, u32[]{:S(2)}) collective-permute-start(bf16[128,2048]{1,0:T(8,128)(2,1)S(1)} %fusion.54), channel_id=1, source_target_pairs={{0,4},{4,8},{8,12},{12,16},{16,20},{20,24},{24,28},{1,5},{5,9},{9,... | collective-permute-start | bytes 1572872 | tf_op jit(solution)/shard_map/while/body/eval_jaxpr/ppermute | solution.py:16
  249.9 11.4 %collective-permute-start = (bf16[128,2048]{1,0:T(8,128)(2,1)S(1)}, bf16[128,2048]{1,0:T(8,128)(2,1)S(1)}, u32[]{:S(2)}, u32[]{:S(2)}) collective-permute-start(bf16[128,2048]{1,0:T(8,128)(2,1)S(1)} %fusion.54), channel_id=1, source_target_pairs={{0,4},{4,8},{8,12},{12,16},{16,20},{20,24},{24,28},{1,5},{5,9},{9,... | collective-permute-start | bytes 1572872 | tf_op jit(solution)/shard_map/while/body/eval_jaxpr/ppermute | solution.py:16
  265.9 11.4 %collective-permute-start = (bf16[128,2048]{1,0:T(8,128)(2,1)S(1)}, bf16[128,2048]{1,0:T(8,128)(2,1)S(1)}, u32[]{:S(2)}, u32[]{:S(2)}) collective-permute-start(bf16[128,2048]{1,0:T(8,128)(2,1)S(1)} %fusion.54), channel_id=1, source_target_pairs={{0,4},{4,8},{8,12},{12,16},{16,20},{20,24},{24,28},{1,5},{5,9},{9,... | collective-permute-start | bytes 1572872 | tf_op jit(solution)/shard_map/while/body/eval_jaxpr/ppermute | solution.py:16
  281.3 3.1 copy-start.18
  284.5 12.1 %collective-permute-start.1 = (bf16[128,2048]{1,0:T(8,128)(2,1)S(1)}, bf16[128,2048]{1,0:T(8,128)(2,1)S(1)}, u32[]{:S(2)}, u32[]{:S(2)}) collective-permute-start(bf16[128,2048]{1,0:T(8,128)(2,1)S(1)} %fusion.61), channel_id=1, source_target_pairs={{4,0},{8,4},{12,8},{16,12},{20,16},{24,20},{28,24},{5,1},{9,5},{13... | collective-permute-start | bytes 1572872 | tf_op jit(solution)/shard_map/while/body/eval_jaxpr/ppermute | solution.py:16
  297.4 2.6 copy-start.17
  300.5 3.1 copy-start.18
  303.7 11.4 %collective-permute-start.1 = (bf16[128,2048]{1,0:T(8,128)(2,1)S(1)}, bf16[128,2048]{1,0:T(8,128)(2,1)S(1)}, u32[]{:S(2)}, u32[]{:S(2)}) collective-permute-start(bf16[128,2048]{1,0:T(8,128)(2,1)S(1)} %fusion.61), channel_id=1, source_target_pairs={{4,0},{8,4},{12,8},{16,12},{20,16},{24,20},{28,24},{5,1},{9,5},{13... | collective-permute-start | bytes 1572872 | tf_op jit(solution)/shard_map/while/body/eval_jaxpr/ppermute | solution.py:16
  315.9 2.6 copy-start.17
  319.0 3.1 copy-start.18
  322.1 11.4 %collective-permute-start.1 = (bf16[128,2048]{1,0:T(8,128)(2,1)S(1)}, bf16[128,2048]{1,0:T(8,128)(2,1)S(1)}, u32[]{:S(2)}, u32[]{:S(2)}) collective-permute-start(bf16[128,2048]{1,0:T(8,128)(2,1)S(1)} %fusion.61), channel_id=1, source_target_pairs={{4,0},{8,4},{12,8},{16,12},{20,16},{24,20},{28,24},{5,1},{9,5},{13... | collective-permute-start | bytes 1572872 | tf_op jit(solution)/shard_map/while/body/eval_jaxpr/ppermute | solution.py:16
  334.3 2.6 copy-start.17
  337.4 3.1 copy-start.18
  340.6 11.4 %collective-permute-start.1 = (bf16[128,2048]{1,0:T(8,128)(2,1)S(1)}, bf16[128,2048]{1,0:T(8,128)(2,1)S(1)}, u32[]{:S(2)}, u32[]{:S(2)}) collective-permute-start(bf16[128,2048]{1,0:T(8,128)(2,1)S(1)} %fusion.61), channel_id=1, source_target_pairs={{4,0},{8,4},{12,8},{16,12},{20,16},{24,20},{28,24},{5,1},{9,5},{13... | collective-permute-start | bytes 1572872 | tf_op jit(solution)/shard_map/while/body/eval_jaxpr/ppermute | solution.py:16
  355.8 3.1 copy-start.18
  359.0 11.4 %collective-permute-start.1 = (bf16[128,2048]{1,0:T(8,128)(2,1)S(1)}, bf16[128,2048]{1,0:T(8,128)(2,1)S(1)}, u32[]{:S(2)}, u32[]{:S(2)}) collective-permute-start(bf16[128,2048]{1,0:T(8,128)(2,1)S(1)} %fusion.61), channel_id=1, source_target_pairs={{4,0},{8,4},{12,8},{16,12},{20,16},{24,20},{28,24},{5,1},{9,5},{13... | collective-permute-start | bytes 1572872 | tf_op jit(solution)/shard_map/while/body/eval_jaxpr/ppermute | solution.py:16
  374.3 3.1 copy-start.18
  377.4 11.4 %collective-permute-start.1 = (bf16[128,2048]{1,0:T(8,128)(2,1)S(1)}, bf16[128,2048]{1,0:T(8,128)(2,1)S(1)}, u32[]{:S(2)}, u32[]{:S(2)}) collective-permute-start(bf16[128,2048]{1,0:T(8,128)(2,1)S(1)} %fusion.61), channel_id=1, source_target_pairs={{4,0},{8,4},{12,8},{16,12},{20,16},{24,20},{28,24},{5,1},{9,5},{13... | collective-permute-start | bytes 1572872 | tf_op jit(solution)/shard_map/while/body/eval_jaxpr/ppermute | solution.py:16
  392.7 3.1 copy-start.18
  395.9 11.4 %collective-permute-start.1 = (bf16[128,2048]{1,0:T(8,128)(2,1)S(1)}, bf16[128,2048]{1,0:T(8,128)(2,1)S(1)}, u32[]{:S(2)}, u32[]{:S(2)}) collective-permute-start(bf16[128,2048]{1,0:T(8,128)(2,1)S(1)} %fusion.61), channel_id=1, source_target_pairs={{4,0},{8,4},{12,8},{16,12},{20,16},{24,20},{28,24},{5,1},{9,5},{13... | collective-permute-start | bytes 1572872 | tf_op jit(solution)/shard_map/while/body/eval_jaxpr/ppermute | solution.py:16
  411.2 3.1 copy-start.18
  414.3 11.4 %collective-permute-start.1 = (bf16[128,2048]{1,0:T(8,128)(2,1)S(1)}, bf16[128,2048]{1,0:T(8,128)(2,1)S(1)}, u32[]{:S(2)}, u32[]{:S(2)}) collective-permute-start(bf16[128,2048]{1,0:T(8,128)(2,1)S(1)} %fusion.61), channel_id=1, source_target_pairs={{4,0},{8,4},{12,8},{16,12},{20,16},{24,20},{28,24},{5,1},{9,5},{13... | collective-permute-start | bytes 1572872 | tf_op jit(solution)/shard_map/while/body/eval_jaxpr/ppermute | solution.py:16
  467.4 18.9 %all-to-all-start.6 = ((f32[1,2048,128]{2,0,1:T(1,128)}), f32[1,2048,128]{2,0,1:T(1,128)S(1)}, u32[]{:S(2)}, u32[]{:S(2)}) async-start(f32[1,2048,128]{2,0,1:T(1,128)} %bitcast.131), calls=%async_computation.6 | async-start | bytes 2097152 | tf_op jit(solution)/shard_map/all_to_all | solution.py:101
  472.5 100.1 %reduce-scatter.7.cloned.1.call-start = ((), (), s32[]{:S(2)}) async-start(), calls=%async_computation.16 | async-start | bytes 2621440
  478.1 10.0 %copy-start.19 = (bf16[1,128,512]{2,1,0:T(8,128)(2,1)S(1)}, bf16[1,128,512]{2,1,0:T(8,128)(2,1)}, u32[]{:S(2)}) copy-start(bf16[1,128,512]{2,1,0:T(8,128)(2,1)} %get-tuple-element.492) | copy-start | bytes 393220
  550.4 19.0 %all-to-all-start.3 = ((f32[8,256,128]{2,1,0:T(8,128)}), f32[8,256,128]{2,1,0:T(8,128)S(1)}, u32[]{:S(2)}, u32[]{:S(2)}) async-start(f32[8,256,128]{2,1,0:T(8,128)} %get-tuple-element.638), calls=%async_computation.3 | async-start | bytes 2097152 | tf_op jit(solution)/shard_map/all_to_all | solution.py:108
  556.2 3.4 copy-start.12
  559.7 14.2 %copy-start.9 = (bf16[8,256,128]{2,1,0:T(8,128)(2,1)S(1)}, bf16[8,256,128]{2,1,0:T(8,128)(2,1)}, u32[]{:S(2)}) copy-start(bf16[8,256,128]{2,1,0:T(8,128)(2,1)} %all_to_all.127) | copy-start | bytes 1572868
  570.4 3.5 copy-start.13
  573.9 3.5 copy-start.8
  573.9 3.5 copy-start.14
  (72 other events, 123.4 us)
Sparse Core Ops, SparseCore 0:
  60.3 44.3 all-gather.2
  106.3 44.4 all-gather.4
  430.9 41.3 reduce-scatter.8
  491.5 41.7 reduce-scatter.6
where the time goes:
time: 593 us; the launch traced here: 586 us
  waiting for transfers between devices  236 us (40%)
  blocking collectives  115 us (19%)
  starting transfers between devices  82 us (14%)
  other arithmetic  62 us (10%)
  local copies, waits for them, and re-layouts  45 us (8%)
  matrix products  29.4 us (5%)
  between operations  14.6 us (2%)
    ppermute x16, waiting for transfers between devices, passed_along(): return lax.ppermute(block, axis, route)  124 us
    ppermute x16, starting transfers between devices, passed_along(): return lax.ppermute(block, axis, route)  56.2 us
    all_gather x1, waiting for transfers between devices, body(): lax.all_gather(output_local, 'tp', axis=1, tiled=True)  46 us
    all_gather x1, waiting for transfers between devices, body(): lax.all_gather(value_local, 'tp', axis=1, tiled=True)  24.8 us
    while x160, local copies, waits for them, and re-layouts  23.1 us
    select_n x8, other arithmetic, backward_step(): jnp.where(active, lax.dynamic_update_index_in_dim(saved_grad, flowing, bl...  19 us
    all_to_all x1, blocking collectives, body(): lax.all_to_all(value_first, 'section', split_axis=1, concat_axis=0, tiled...  18.9 us
    all_to_all x1, blocking collectives, body(): lax.all_to_all(chosen[4], 'section', split_axis=0, concat_axis=1, tiled=T...  18.4 us
  transfers between devices with their start and end apart: 25, of which 22 were waited for; matrix products, arithmetic and copies ran while one was open for 17% of the time, Pallas kernels for 0%

commit v1 on v0

--- a/solution.py
+++ b/solution.py
@@ -1,6 +1,10 @@
+import functools
+
 import jax
 import jax.numpy as jnp
 from jax import lax
+from jax.experimental import pallas as pl
+from jax.experimental.pallas import tpu as pltpu
 from jax.sharding import PartitionSpec as P
 
 epsilon = 1e-05
@@ -62,7 +66,7 @@
     return (weight_new[None], first_new[None], second_new[None])
 
 
-def body(
+def cascade_body(
     tokens,
     cotangent,
     value_weight,
@@ -218,6 +222,279 @@
     return (value_new[0], output_new[0], value_new[1], output_new[1], value_new[2], output_new[2])
 
 
+vmem_budget = 58 * 2**20
+
+
+def layer_tables(layer_map, old_section, new_section, sections):
+    positions = lax.iota(jnp.int32, sections)
+    owner_match = new_section[None, :] == positions[:, None]
+    has_layer = jnp.any(owner_match, axis=1)
+    new_index = jnp.sum(
+        jnp.where(owner_match, lax.iota(jnp.int32, new_section.shape[0])[None, :], 0), axis=1
+    )
+    map_match = new_index[:, None] == lax.iota(jnp.int32, layer_map.shape[0])[None, :]
+    old_index = jnp.sum(jnp.where(map_match, layer_map[None, :], 0), axis=1)
+    section_match = old_index[:, None] == lax.iota(jnp.int32, old_section.shape[0])[None, :]
+    source = jnp.sum(jnp.where(section_match, old_section[None, :], 0), axis=1)
+    return (has_layer, jnp.where(has_layer, new_index, -1), source)
+
+
+def exchanged(block, mask):
+    sections = lax.axis_size("section")
+    return lax.ppermute(block, "section", [(i, i ^ mask) for i in range(sections)])
+
+
+def rotated(block, distance):
+    count = lax.axis_size("tp")
+    return lax.ppermute(block, "tp", [(i, (i + distance) % count) for i in range(count)])
+
+
+def token_share(block):
+    sections, count = lax.axis_size("section"), lax.axis_size("tp")
+    share = count // 2
+    parts = []
+    for slot in range(share):
+        route = [
+            (s * count + z, s * count + (z + slot + (s % 2) * share) % count)
+            for s in range(sections)
+            for z in range(count)
+        ]
+        parts.append(lax.ppermute(block, ("section", "tp"), route))
+    return jnp.concatenate(parts, axis=0)
+
+
+def gathered_pieces(block):
+    sections, count = lax.axis_size("section"), lax.axis_size("tp")
+    column = jnp.stack([block] + [rotated(block, r) for r in range(1, count)], axis=1)
+    bits = [1 << b for b in range(1, sections.bit_length() - 1)]
+    joint = {0: column}
+    for bit in bits:
+        joint[bit] = exchanged(column, bit)
+    values = {m: joint[m][0] for m in joint}
+    outputs = {m: joint[m][1] for m in joint}
+    single_value, single_output = {}, {}
+    for mask in range(2, sections, 2):
+        if mask in joint:
+            continue
+        high = 1 << (mask.bit_length() - 1)
+        low = mask & -mask
+        values[mask] = single_value[mask] = exchanged(values[mask ^ high], high)
+    for mask in sorted(range(2, sections, 2), key=lambda m: bin(m).count("1")):
+        if mask in joint:
+            continue
+        low = mask & -mask
+        outputs[mask] = single_output[mask] = exchanged(outputs[mask ^ low], low)
+    for part in (joint, single_value, single_output):
+        for mask in list(part):
+            part[mask ^ 1] = exchanged(part[mask], 1)
+    return (joint, single_value, single_output)
+
+
+def stack_kernel(layout, sizes, table_ref, tokens_ref, cotangent_ref, *refs):
+    layers, old, sections, count, depth = sizes
+    pieces = refs[: len(layout)]
+    grads_ref, local_ref, value, output, streams, preacts, units, flowing, sems = refs[len(layout) :]
+    myself = table_ref[layers + 2]
+    mytp = table_ref[layers + 3]
+    rows = depth // sections
+    channels = value.shape[2]
+    width = channels // count
+    for place, (mask, matrices, first, number) in enumerate(layout):
+        slab = jnp.bitwise_xor(myself, mask)
+        row_at = pl.ds(pl.multiple_of(slab * rows, rows), rows)
+        for index in range(number):
+            for rotation in range(count):
+                owner = lax.rem(mytp - rotation + count, count)
+                lane_at = pl.ds(pl.multiple_of(owner * width, width), width)
+                for order, matrix in enumerate(matrices):
+                    target = (value, output)[matrix]
+                    piece = pieces[place]
+                    source = piece.at[order, rotation, index] if len(matrices) > 1 else piece.at[rotation, index]
+                    pltpu.make_async_copy(
+                        source, target.at[first + index, row_at, lane_at], sems.at[matrix, first + index]
+                    ).start()
+    streams[0] = tokens_ref[...]
+    flowing[...] = cotangent_ref[...]
+    grads_ref[...] = jnp.zeros_like(grads_ref)
+    local_ref[...] = jnp.zeros_like(local_ref)
+
+    def forward(j, carry):
+        old_layer = table_ref[j]
+        before = table_ref[jnp.maximum(j - 1, 0)]
+
+        @pl.when((j == 0) | (before != old_layer))
+        def _():
+            for matrix, target in enumerate((value, output)):
+                pltpu.make_async_copy(
+                    target.at[old_layer], target.at[old_layer], sems.at[matrix, old_layer]
+                ).wait()
+
+        stream = streams[j].astype(jnp.float32)
+        factor = lax.rsqrt(jnp.mean(stream * stream, axis=-1, keepdims=True) + epsilon)
+        hidden = (stream * factor).astype(jnp.bfloat16)
+        preact = jnp.dot(hidden, value[old_layer], preferred_element_type=jnp.float32)
+        unit_values = (preact / (1.0 + jnp.exp(-preact))).astype(jnp.bfloat16)
+        preacts[j] = preact
+        units[j] = unit_values
+
+        @pl.when(j < layers - 1)
+        def _():
+            mixing = lax.dot_general(
+                unit_values, output[old_layer], (((1,), (1,)), ((), ())), preferred_element_type=jnp.float32
+            )
+            streams[j + 1] = (streams[j].astype(jnp.float32) + mixing).astype(jnp.bfloat16)
+
+        return carry
+
+    lax.fori_loop(0, layers, forward, 0)
+    mine_at = pl.ds(pl.multiple_of(mytp * width, width), width)
+
+    def backward(step, carry):
+        j = layers - 1 - step
+        old_layer = table_ref[j]
+        grad_out = flowing[...]
+        grad_units = jnp.dot(grad_out, output[old_layer], preferred_element_type=jnp.float32)
+        preact = preacts[j]
+        gate_value = 1.0 / (1.0 + jnp.exp(-preact))
+        grad_inner = (grad_units * gate_value * (1.0 + preact * (1.0 - gate_value))).astype(jnp.bfloat16)
+        preacts[j] = grad_inner.astype(jnp.float32)
+        stream = streams[j].astype(jnp.float32)
+        factor = lax.rsqrt(jnp.mean(stream * stream, axis=-1, keepdims=True) + epsilon)
+        normed = stream * factor
+        for which in range(2):
+
+            @pl.when(table_ref[layers + which] == j)
+            def _():
+                inner = preacts[j, :, mine_at].astype(jnp.bfloat16)
+                grads_ref[which, 0] = lax.dot_general(
+                    normed.astype(jnp.bfloat16), inner, (((0,), (0,)), ((), ())), preferred_element_type=jnp.float32
+                )
+                grads_ref[which, 1] = lax.dot_general(
+                    grad_out, units[j, :, mine_at], (((0,), (0,)), ((), ())), preferred_element_type=jnp.float32
+                )
+                if which == 0:
+                    local_ref[0] = value[old_layer, :, mine_at]
+                    local_ref[1] = output[old_layer, :, mine_at]
+
+        @pl.when(j > 0)
+        def _():
+            grad_hidden = lax.dot_general(
+                grad_inner, value[old_layer], (((1,), (1,)), ((), ())), preferred_element_type=jnp.float32
+            )
+            mean = jnp.mean(grad_hidden * normed, axis=-1, keepdims=True)
+            flowing[...] = (
+                flowing[...].astype(jnp.float32) + factor * (grad_hidden - normed * mean)
+            ).astype(jnp.bfloat16)
+
+        return carry
+
+    lax.fori_loop(0, layers, backward, 0)
+
+
+def replicated_body(
+    tokens,
+    cotangent,
+    value_weight,
+    output_weight,
+    value_first,
+    output_first,
+    value_second,
+    output_second,
+    layer_map,
+    old_section,
+    new_section,
+):
+    sections, count = lax.axis_size("section"), lax.axis_size("tp")
+    myself, mytp = lax.axis_index("section"), lax.axis_index("tp")
+    layers, old = layer_map.shape[0], old_section.shape[0]
+    depth, width = value_weight.shape[1:]
+    rows = depth // sections
+    has_layer, owned, source = layer_tables(layer_map, old_section, new_section, sections)
+
+    my_tokens = token_share(tokens)
+    weights = jnp.concatenate(
+        [value_weight.reshape(sections, 1, rows, width), output_weight.reshape(sections, 1, rows, width)], axis=1
+    )
+    spread = lax.all_to_all(weights, "section", split_axis=0, concat_axis=0, tiled=True)
+    chosen = jnp.stack([lax.dynamic_index_in_dim(spread, old_section[i], 0, False) for i in range(old)], axis=1)
+    chunks = 2 if old % 2 == 0 else 1
+    number = old // chunks
+    layout, pieces = [], []
+    for chunk in range(chunks):
+        first = chunk * number
+        joint, single_value, single_output = gathered_pieces(chosen[:, first : first + number])
+        for part, matrices in ((joint, (0, 1)), (single_value, (0,)), (single_output, (1,))):
+            for mask in part:
+                layout.append((mask, matrices, first, number))
+                pieces.append(part[mask])
+    my_cotangent = token_share(cotangent)
+
+    moments = jnp.stack(
+        [m.astype(jnp.bfloat16).reshape(sections, rows, width) for m in (value_first, output_first, value_second, output_second)],
+        axis=1,
+    )
+    moments = lax.all_to_all(moments, "section", split_axis=0, concat_axis=0, tiled=True)
+    moments = jnp.stack([lax.dynamic_index_in_dim(moments, source[i], 0, False) for i in range(sections)])
+    moments = lax.all_to_all(moments, "section", split_axis=0, concat_axis=0, tiled=True)
+    moments = moments.transpose(1, 0, 2, 3).reshape(4, depth, width).astype(jnp.float32)
+    holds = has_layer[myself].astype(jnp.float32)
+    moments = moments * holds
+
+    table = jnp.concatenate(
+        [layer_map, jnp.stack([owned[myself], owned[jnp.bitwise_xor(myself, 1)], myself, mytp])]
+    ).astype(jnp.int32)
+    share = my_tokens.shape[0]
+    channels = width * count
+    any_space = pl.BlockSpec(memory_space=pl.ANY)
+    vmem_space = pl.BlockSpec(memory_space=pltpu.VMEM)
+    grads, local = pl.pallas_call(
+        functools.partial(stack_kernel, tuple(layout), (layers, old, sections, count, depth)),
+        in_specs=[pl.BlockSpec(memory_space=pltpu.SMEM), vmem_space, vmem_space] + [any_space] * len(pieces),
+        out_specs=[vmem_space, vmem_space],
+        out_shape=[
+            jax.ShapeDtypeStruct((2, 2, depth, width), jnp.float32),
+            jax.ShapeDtypeStruct((2, depth, width), jnp.bfloat16),
+        ],
+        scratch_shapes=[
+            pltpu.VMEM((old, depth, channels), jnp.bfloat16),
+            pltpu.VMEM((old, depth, channels), jnp.bfloat16),
+            pltpu.VMEM((layers, share, depth), jnp.bfloat16),
+            pltpu.VMEM((layers, share, channels), jnp.float32),
+            pltpu.VMEM((layers, share, channels), jnp.bfloat16),
+            pltpu.VMEM((share, depth), jnp.bfloat16),
+            pltpu.SemaphoreType.DMA((2, old)),
+        ],
+        compiler_params=pltpu.CompilerParams(vmem_limit_bytes=vmem_budget),
+        cost_estimate=pl.CostEstimate(
+            flops=9 * layers * share * depth * channels, bytes_accessed=4 * old * depth * channels, transcendentals=0
+        ),
+        name="stack",
+    )(table, my_tokens, my_cotangent, *pieces)
+    gradient = grads[0] + exchanged(grads[1].astype(jnp.bfloat16), 1).astype(jnp.float32)
+    value_new = adam_update(local[0], moments[0], moments[2], gradient[0])
+    output_new = adam_update(local[1], moments[1], moments[3], gradient[1])
+    return (value_new[0], output_new[0], value_new[1], output_new[1], value_new[2], output_new[2])
+
+
+def chip_need(layers, old, share, depth, channels):
+    weights = 4 * old * depth * channels
+    kept = layers * share * (2 * depth + 6 * channels)
+    return weights + kept + 14 * share * depth
+
+
+def body(*arguments):
+    tokens, value_weight, layer_map, old_section = arguments[0], arguments[2], arguments[8], arguments[9]
+    sections, count = lax.axis_size("section"), lax.axis_size("tp")
+    depth, width = value_weight.shape[1:]
+    need = chip_need(
+        layer_map.shape[0], old_section.shape[0], tokens.shape[0] * count // 2, depth, width * count
+    )
+    even = sections & (sections - 1) == 0 and sections > 1 and count % 2 == 0
+    if even and depth % sections == 0 and need <= vmem_budget:
+        return replicated_body(*arguments)
+    return cascade_body(*arguments)
+
+
 def solution(mesh):
     placed = (
         P("tp", None),

time: 593 us -> 232 us (0.39)
  waiting for transfers between devices: 236 us -> 96.7 us
  blocking collectives: 115 us -> 0 us
  other arithmetic: 62 us -> 13.5 us
  starting transfers between devices: 82 us -> 41.1 us
  Pallas kernels: 0 us -> 30.8 us
  matrix products: 29.4 us -> 0 us
  local copies, waits for them, and re-layouts: 45 us -> 23.3 us
  between operations: 14.6 us -> 24.8 us
    all_to_all x7 -> x0, blocking collectives: 115 us -> none  [the longest x1 18.9 us: body(): lax.all_to_all(value_first, 'section', split_axis=1, concat_axis=0, tiled...]
    all_gather x2 -> x0, waiting for transfers between devices: 70.8 us -> none  [the longest x1 46 us: body(): lax.all_gather(output_local, 'tp', axis=1, tiled=True)]
    select_n x33 -> x1, other arithmetic: 40.1 us -> 0.01 us  [layer_tables(): return (has_layer, jnp.where(has_layer, new_index, -1), source)]
    all_to_all x5 -> x3, waiting for transfers between devices: 41.1 us -> 5.46 us  [the longest x1 5.45 us: replicated_body(): lax.all_to_all(weights, 'section', split_axis=0, concat_axis=0, tiled=True)]
    ppermute x16 -> x29, waiting for transfers between devices: 124 us -> 91.2 us  [the longest x19 41.6 us: exchanged(): lax.ppermute(block, 'section', [(i, i ^ mask) for i in range(sections)])]
    pallas_call x0 -> x1, Pallas kernels: none -> 30.8 us  [replicated_body(): pl.pallas_call(functools.partial(stack_kernel, tuple(layout), (layers, ol...]
    dot_general x34 -> x0, matrix products: 29.4 us -> none  [the longest x8 11.6 us: forward_layer(): lax.dot_general(unit_values, output_full, (((1,), (1,)), ((), ())), prefe...]
    ppermute x16 -> x29, starting transfers between devices: 56.2 us -> 27.7 us  [the longest x19 12.4 us: exchanged(): lax.ppermute(block, 'section', [(i, i ^ mask) for i in range(sections)])]
  transfers between devices with their start and end apart: 25 -> 32, of which waited for: 22 -> 13; matrix products, arithmetic and copies ran while one was open for 17% -> 12% of each run, Pallas kernels for 0% -> 13%
where the time goes in v1:
time: 232 us; the launch traced here: 230 us
  waiting for transfers between devices  96.7 us (42%)
  starting transfers between devices  41.1 us (18%)
  Pallas kernels  30.8 us (13%)
  between operations  24.8 us (11%)
  local copies, waits for them, and re-layouts  23.3 us (10%)
  other arithmetic  13.5 us (6%)
    ppermute x19, waiting for transfers between devices, exchanged(): lax.ppermute(block, 'section', [(i, i ^ mask) for i in range(sections)])  41.6 us
    ppermute x6, waiting for transfers between devices, rotated(): lax.ppermute(block, 'tp', [(i, (i + distance) % count) for i in range(cou...  39.9 us
    pallas_call x1, Pallas kernels, replicated_body(): pl.pallas_call(functools.partial(stack_kernel, tuple(layout), (layers, ol...  30.8 us
    ppermute x19, starting transfers between devices, exchanged(): lax.ppermute(block, 'section', [(i, i ^ mask) for i in range(sections)])  12.4 us
    ppermute x4, starting transfers between devices, token_share(): parts.append(lax.ppermute(block, ('section', 'tp'), route))  9.99 us
    ppermute x4, waiting for transfers between devices, token_share(): parts.append(lax.ppermute(block, ('section', 'tp'), route))  9.77 us
    all_to_all x2, starting transfers between devices, replicated_body(): lax.all_to_all(moments, 'section', split_axis=0, concat_axis=0, tiled=True)  8.89 us
    unnamed x41, local copies, waits for them, and re-layouts  8.79 us
  transfers between devices with their start and end apart: 32, of which 13 were waited for; matrix products, arithmetic and copies ran while one was open for 12% of the time, Pallas kernels for 13%

profile of v1, /device:TPU:19, one launch (start us, length us, event | category | flops | bytes accessed | tf_op | source)
XLA Modules:
  0.0 230.3 jit_solution(1458240823463323105)
XLA Ops:
  0.6 2.3 pad_maximum_fusion.3
  2.9 4.5 %all-to-all-start = ((bf16[8,2,256,128]{3,2,1,0:T(8,128)(2,1)}), bf16[8,2,256,128]{3,2,1,0:T(8,128)(2,1)S(1)}, u32[]{:S(2)}, u32[]{:S(2)}) async-start(bf16[8,2,256,128]{3,2,1,0:T(8,128)(2,1)} %pad_maximum_fusion.3), calls=%async_computation | async-start | bytes 2097152 | tf_op jit(solution)/shard_map/all_to_all | solution.py:418
  15.8 5.5 %all-to-all-done = bf16[8,2,256,128]{3,2,1,0:T(8,128)(2,1)S(1)} async-done(((bf16[8,2,256,128]{3,2,1,0:T(8,128)(2,1)}), bf16[8,2,256,128]{3,2,1,0:T(8,128)(2,1)S(1)}, u32[]{:S(2)}, u32[]{:S(2)}) %all-to-all-start) | async-done | bytes 1048608 | tf_op jit(solution)/shard_map/all_to_all | solution.py:418
  21.4 1.3 collective-permute-start.16
  22.8 1.2 collective-permute-start.18
  24.3 2.3 %collective-permute-start.5 = (bf16[2,2,256,128]{3,2,1,0:T(8,128)(2,1)S(1)}, bf16[2,2,256,128]{3,2,1,0:T(8,128)(2,1)S(1)}, u32[]{:S(2)}, u32[]{:S(2)}) collective-permute-start(bf16[2,2,256,128]{3,2,1,0:T(8,128)(2,1)S(1)} %get-tuple-element.30), channel_id=1, source_target_pairs={{0,2},{1,3},{2,0},{3,1},{4,6},{5,7},{6,4},{7,5},{8,10},{9,11},{10,... | collective-permute-start | bytes 786440 | tf_op jit(solution)/shard_map/ppermute | solution.py:249
  26.6 2.3 collective-permute-done.16
  29.0 11.0 %collective-permute-done.17 = bf16[2,2,256,128]{3,2,1,0:T(8,128)(2,1)S(1)} collective-permute-done((bf16[2,2,256,128]{3,2,1,0:T(8,128)(2,1)S(1)}, bf16[2,2,256,128]{3,2,1,0:T(8,128)(2,1)S(1)}, u32[]{:S(2)}, u32[]{:S(2)}) %collective-permute-start.17) | collective-permute-done | bytes 262176 | tf_op jit(solution)/shard_map/ppermute | solution.py:249
  40.0 5.5 %collective-permute-start = (bf16[128,2048]{1,0:T(8,128)(2,1)}, bf16[128,2048]{1,0:T(8,128)(2,1)}, u32[]{:S(2)}, u32[]{:S(2)}) collective-permute-start(bf16[128,2048]{1,0:T(8,128)(2,1)} %param.11), channel_id=1, source_target_pairs={{0,0},{1,1},{2,2},{3,3},{4,6},{5,7},{6,4},{7,5},{8,8},{9,9},{10,10... | collective-permute-start | bytes 1572872 | tf_op jit(solution)/shard_map/ppermute | solution.py:262
  45.5 11.3 %collective-permute-done.18 = bf16[2,2,256,128]{3,2,1,0:T(8,128)(2,1)S(1)} collective-permute-done((bf16[2,2,256,128]{3,2,1,0:T(8,128)(2,1)S(1)}, bf16[2,2,256,128]{3,2,1,0:T(8,128)(2,1)S(1)}, u32[]{:S(2)}, u32[]{:S(2)}) %collective-permute-start.18) | collective-permute-done | bytes 262176 | tf_op jit(solution)/shard_map/ppermute | solution.py:249
  57.0 1.3 collective-permute-start.19
  58.2 10.0 %collective-permute-done.4 = bf16[2,2,256,128]{3,2,1,0:T(8,128)(2,1)S(1)} collective-permute-done((bf16[2,2,256,128]{3,2,1,0:T(8,128)(2,1)S(1)}, bf16[2,2,256,128]{3,2,1,0:T(8,128)(2,1)S(1)}, u32[]{:S(2)}, u32[]{:S(2)}) %collective-permute-start.4) | collective-permute-done | bytes 262176 | tf_op jit(solution)/shard_map/ppermute | solution.py:249
  68.3 5.2 %collective-permute-done.6 = bf16[2,2,256,128]{3,2,1,0:T(8,128)(2,1)S(1)} collective-permute-done((bf16[2,2,256,128]{3,2,1,0:T(8,128)(2,1)S(1)}, bf16[2,2,256,128]{3,2,1,0:T(8,128)(2,1)S(1)}, u32[]{:S(2)}, u32[]{:S(2)}) %collective-permute-start.6) | collective-permute-done | bytes 262176 | tf_op jit(solution)/shard_map/ppermute | solution.py:249
  73.5 1.1 pad_maximum_fusion.4.refs_0_
  75.1 0.7 copy-done.5
  75.9 3.4 %collective-permute-done = bf16[128,2048]{1,0:T(8,128)(2,1)} collective-permute-done((bf16[128,2048]{1,0:T(8,128)(2,1)}, bf16[128,2048]{1,0:T(8,128)(2,1)}, u32[]{:S(2)}, u32[]{:S(2)}) %collective-permute-start) | collective-permute-done | bytes 524320 | tf_op jit(solution)/shard_map/ppermute | solution.py:262
  79.7 1.6 pad_maximum_fusion
  81.3 5.2 %all-to-all-start.1 = ((bf16[8,4,256,128]{3,2,1,0:T(8,128)(2,1)}), bf16[8,4,256,128]{3,2,1,0:T(8,128)(2,1)S(1)}, u32[]{:S(2)}, u32[]{:S(2)}) async-start(bf16[8,4,256,128]{3,2,1,0:T(8,128)(2,1)} %pad_maximum_fusion), calls=%async_computation.1 | async-start | bytes 4194304 | tf_op jit(solution)/shard_map/all_to_all | solution.py:436
  86.8 6.4 %collective-permute-done.1 = bf16[128,2048]{1,0:T(8,128)(2,1)} collective-permute-done((bf16[128,2048]{1,0:T(8,128)(2,1)}, bf16[128,2048]{1,0:T(8,128)(2,1)}, u32[]{:S(2)}, u32[]{:S(2)}) %collective-permute-start.1) | collective-permute-done | bytes 524320 | tf_op jit(solution)/shard_map/ppermute | solution.py:262
  94.5 1.1 slice_bitcast_fusion.1
  95.6 4.1 %collective-permute-start.2 = (bf16[128,2048]{1,0:T(8,128)(2,1)}, bf16[128,2048]{1,0:T(8,128)(2,1)S(1)}, u32[]{:S(2)}, u32[]{:S(2)}) collective-permute-start(bf16[128,2048]{1,0:T(8,128)(2,1)} %param.12), channel_id=1, source_target_pairs={{0,0},{1,1},{2,2},{3,3},{4,6},{5,7},{6,4},{7,5},{8,8},{9,9},{10,10... | collective-permute-start | bytes 1572872 | tf_op jit(solution)/shard_map/ppermute | solution.py:262
  99.7 3.7 %collective-permute-done.7.refs_1_ = bf16[2,4,2,256,128]{4,3,2,1,0:T(8,128)(2,1)} collective-permute-done((bf16[2,4,2,256,128]{4,3,2,1,0:T(8,128)(2,1)}, bf16[2,4,2,256,128]{4,3,2,1,0:T(8,128)(2,1)}, u32[]{:S(2)}, u32[]{:S(2)}) %collective-permute-start.7) | collective-permute-done | bytes 1048608 | tf_op jit(solution)/shard_map/ppermute | solution.py:244
  103.4 21.3 %collective-permute-done.8.refs_2_ = bf16[2,4,2,256,128]{4,3,2,1,0:T(8,128)(2,1)} collective-permute-done((bf16[2,4,2,256,128]{4,3,2,1,0:T(8,128)(2,1)}, bf16[2,4,2,256,128]{4,3,2,1,0:T(8,128)(2,1)}, u32[]{:S(2)}, u32[]{:S(2)}) %collective-permute-start.8) | collective-permute-done | bytes 1048608 | tf_op jit(solution)/shard_map/ppermute | solution.py:244
  124.7 1.9 slice_bitcast_fusion
  126.6 1.9 slice_bitcast_fusion.3
  128.5 1.9 slice_bitcast_fusion.2
  130.4 1.5 collective-permute-start.12
  131.9 1.4 collective-permute-start.14
  133.3 13.9 %collective-permute-done.24.refs_16_ = bf16[4,2,256,128]{3,2,1,0:T(8,128)(2,1)} collective-permute-done((bf16[4,2,256,128]{3,2,1,0:T(8,128)(2,1)S(1)}, bf16[4,2,256,128]{3,2,1,0:T(8,128)(2,1)}, u32[]{:S(2)}, u32[]{:S(2)}) %collective-permute-start.24) | collective-permute-done | bytes 524320 | tf_op jit(solution)/shard_map/ppermute | solution.py:244
  147.2 5.5 %collective-permute-start.25 = (bf16[4,2,256,128]{3,2,1,0:T(8,128)(2,1)}, bf16[4,2,256,128]{3,2,1,0:T(8,128)(2,1)}, u32[]{:S(2)}, u32[]{:S(2)}) collective-permute-start(bf16[4,2,256,128]{3,2,1,0:T(8,128)(2,1)} %collective-permute-done.24.refs_16_), channel_id=1, source_target_pairs={{0,4},{4,0},{8,12},{12,8},{16,20},{20,16},{24,28},{28,24},{1,5},{5... | collective-permute-start | bytes 1572872 | tf_op jit(solution)/shard_map/ppermute | solution.py:244
  169.1 1.8 concatenate.14.table_ref
  170.9 2.3 pad_maximum_fusion.1.tokens_ref
  174.3 1.0 pad_maximum_fusion.2.cotangent_ref
  175.3 0.7 dynamic-slice_dynamic-update-slice_fusion.7
  176.0 0.7 dynamic-slice_dynamic-update-slice_fusion.6
  176.8 0.7 dynamic-slice_dynamic-update-slice_fusion.5
  177.5 2.5 %collective-permute-done.27.refs_19_ = bf16[4,2,256,128]{3,2,1,0:T(8,128)(2,1)} collective-permute-done((bf16[4,2,256,128]{3,2,1,0:T(8,128)(2,1)}, bf16[4,2,256,128]{3,2,1,0:T(8,128)(2,1)}, u32[]{:S(2)}, u32[]{:S(2)}) %collective-permute-start.27) | collective-permute-done | bytes 524320 | tf_op jit(solution)/shard_map/ppermute | solution.py:244
  180.6 0.7 dynamic-slice_dynamic-update-slice_fusion.4
  181.3 0.7 dynamic-slice_dynamic-update-slice_fusion.3
  182.0 0.7 dynamic-slice_dynamic-update-slice_fusion.2
  182.8 0.7 dynamic-slice_dynamic-update-slice_fusion.1
  183.5 0.7 dynamic-slice_dynamic-update-slice_fusion
  184.2 3.7 %all-to-all-start.2 = ((bf16[8,4,256,128]{3,2,1,0:T(8,128)(2,1)}), bf16[8,4,256,128]{3,2,1,0:T(8,128)(2,1)S(1)}, u32[]{:S(2)}, u32[]{:S(2)}) async-start(bf16[8,4,256,128]{3,2,1,0:T(8,128)(2,1)} %dynamic-slice_dynamic-update-slice_fusion), calls=%async_computation.2 | async-start | bytes 4194304 | tf_op jit(solution)/shard_map/all_to_all | solution.py:438
  188.1 0.7 copy-done.14
  189.0 30.8 %stack.88 = (f32[2,2,2048,128]{3,2,1,0:T(8,128)}, bf16[2,2048,128]{2,1,0:T(8,128)(2,1)}) custom-call(s32[10]{0:T(128)} %concatenate.14.table_ref, bf16[256,2048]{1,0:T(8,128)(2,1)} %pad_maximum_fusion.1.tokens_ref, bf16[256,2048]{1,0:T(8,128)(2,1)} %pad_maximum_fusion.2.cotangent_ref, bf16[2,4,2,256,128]{4,3,2,1,0:T(8,128)(2,1)} %pad_maximum_fusion.4.refs_0_, ...), custom_call_target="tpu_custom_call" | custom-call | flops 14495514624 | bytes 16777216 | tf_op jit(solution)/shard_map/stack/pallas_call | solution.py:450
  219.8 2.7 %fusion.2 = bf16[2,2048,128]{2,1,0:T(8,128)(2,1)} fusion(f32[2,2,2048,128]{3,2,1,0:T(8,128)} %get-tuple-element.9), kind=kLoop, calls=%fused_computation.8 | loop fusion | bytes 2097152 | tf_op jit(solution)/shard_map/convert_element_type | solution.py:473
  225.4 1.4 copy-done
  227.3 3.0 %subtract_convert_fusion = (bf16[1,2048,128]{2,1,0:T(8,128)(2,1)}, f32[1,2048,128]{2,1,0:T(8,128)}, f32[1,2048,128]{2,1,0:T(8,128)}, bf16[1,2048,128]{2,1,0:T(8,...) fusion(bf16[2,2048,128]{2,1,0:T(8,128)(2,1)S(1)} %copy-done.1, f32[1,2048,128]{2,1,0:T(8,128)S(1)} %bitcast.74, ...), kind=kLoop, calls=%fused_computation.18 | loop fusion | flops 5767168 | bytes 12582912 | tf_op jit(solution)/shard_map/convert_element_type | solution.py:65
  (91 shorter events, 9.2 us)
Async XLA Ops:
  0.6 6.8 %copy-start.11 = (s32[4]{0:T(128)S(1)}, s32[4]{0:T(128)}, u32[]{:S(2)}) copy-start(s32[4]{0:T(128)} %param.20) | copy-start | bytes 52
  2.9 18.4 %all-to-all-start = ((bf16[8,2,256,128]{3,2,1,0:T(8,128)(2,1)}), bf16[8,2,256,128]{3,2,1,0:T(8,128)(2,1)S(1)}, u32[]{:S(2)}, u32[]{:S(2)}) async-start(bf16[8,2,256,128]{3,2,1,0:T(8,128)(2,1)} %pad_maximum_fusion.3), calls=%async_computation | async-start | bytes 2097152 | tf_op jit(solution)/shard_map/all_to_all | solution.py:418
  21.4 7.6 %collective-permute-start.16 = (bf16[2,2,256,128]{3,2,1,0:T(8,128)(2,1)S(1)}, bf16[2,2,256,128]{3,2,1,0:T(8,128)(2,1)S(1)}, u32[]{:S(2)}, u32[]{:S(2)}) collective-permute-start(bf16[2,2,256,128]{3,2,1,0:T(8,128)(2,1)S(1)} %get-tuple-element.28), channel_id=1, source_target_pairs={{0,1},{1,2},{2,3},{3,0},{4,5},{5,6},{6,7},{7,4},{8,9},{9,10},{10,1... | collective-permute-start | bytes 786440 | tf_op jit(solution)/shard_map/ppermute | solution.py:249
  22.7 17.3 %collective-permute-start.17 = (bf16[2,2,256,128]{3,2,1,0:T(8,128)(2,1)S(1)}, bf16[2,2,256,128]{3,2,1,0:T(8,128)(2,1)S(1)}, u32[]{:S(2)}, u32[]{:S(2)}) collective-permute-start(bf16[2,2,256,128]{3,2,1,0:T(8,128)(2,1)S(1)} %get-tuple-element.28), channel_id=1, source_target_pairs={{0,2},{1,3},{2,0},{3,1},{4,6},{5,7},{6,4},{7,5},{8,10},{9,11},{10,... | collective-permute-start | bytes 786440 | tf_op jit(solution)/shard_map/ppermute | solution.py:249
  22.8 34.1 %collective-permute-start.18 = (bf16[2,2,256,128]{3,2,1,0:T(8,128)(2,1)S(1)}, bf16[2,2,256,128]{3,2,1,0:T(8,128)(2,1)S(1)}, u32[]{:S(2)}, u32[]{:S(2)}) collective-permute-start(bf16[2,2,256,128]{3,2,1,0:T(8,128)(2,1)S(1)} %get-tuple-element.28), channel_id=1, source_target_pairs={{0,3},{1,0},{2,1},{3,2},{4,7},{5,4},{6,5},{7,6},{8,11},{9,8},{10,9... | collective-permute-start | bytes 786440 | tf_op jit(solution)/shard_map/ppermute | solution.py:249
  24.0 44.3 %collective-permute-start.4 = (bf16[2,2,256,128]{3,2,1,0:T(8,128)(2,1)S(1)}, bf16[2,2,256,128]{3,2,1,0:T(8,128)(2,1)S(1)}, u32[]{:S(2)}, u32[]{:S(2)}) collective-permute-start(bf16[2,2,256,128]{3,2,1,0:T(8,128)(2,1)S(1)} %get-tuple-element.30), channel_id=1, source_target_pairs={{0,1},{1,2},{2,3},{3,0},{4,5},{5,6},{6,7},{7,4},{8,9},{9,10},{10,1... | collective-permute-start | bytes 786440 | tf_op jit(solution)/shard_map/ppermute | solution.py:249
  24.3 44.0 %collective-permute-start.5 = (bf16[2,2,256,128]{3,2,1,0:T(8,128)(2,1)S(1)}, bf16[2,2,256,128]{3,2,1,0:T(8,128)(2,1)S(1)}, u32[]{:S(2)}, u32[]{:S(2)}) collective-permute-start(bf16[2,2,256,128]{3,2,1,0:T(8,128)(2,1)S(1)} %get-tuple-element.30), channel_id=1, source_target_pairs={{0,2},{1,3},{2,0},{3,1},{4,6},{5,7},{6,4},{7,5},{8,10},{9,11},{10,... | collective-permute-start | bytes 786440 | tf_op jit(solution)/shard_map/ppermute | solution.py:249
  28.9 44.6 %collective-permute-start.6 = (bf16[2,2,256,128]{3,2,1,0:T(8,128)(2,1)S(1)}, bf16[2,2,256,128]{3,2,1,0:T(8,128)(2,1)S(1)}, u32[]{:S(2)}, u32[]{:S(2)}) collective-permute-start(bf16[2,2,256,128]{3,2,1,0:T(8,128)(2,1)S(1)} %get-tuple-element.30), channel_id=1, source_target_pairs={{0,3},{1,0},{2,1},{3,2},{4,7},{5,4},{6,5},{7,6},{8,11},{9,8},{10,9... | collective-permute-start | bytes 786440 | tf_op jit(solution)/shard_map/ppermute | solution.py:249
  40.0 39.3 %collective-permute-start = (bf16[128,2048]{1,0:T(8,128)(2,1)}, bf16[128,2048]{1,0:T(8,128)(2,1)}, u32[]{:S(2)}, u32[]{:S(2)}) collective-permute-start(bf16[128,2048]{1,0:T(8,128)(2,1)} %param.11), channel_id=1, source_target_pairs={{0,0},{1,1},{2,2},{3,3},{4,6},{5,7},{6,4},{7,5},{8,8},{9,9},{10,10... | collective-permute-start | bytes 1572872 | tf_op jit(solution)/shard_map/ppermute | solution.py:262
  56.8 17.9 %copy-start.2 = (f32[1,2048,128]{2,1,0:T(8,128)S(1)}, f32[1,2048,128]{2,1,0:T(8,128)}, u32[]{:S(2)}) copy-start(f32[1,2048,128]{2,1,0:T(8,128)} %param.15) | copy-start | bytes 3145732
  57.0 36.3 %copy-start.6 = (bf16[2,4,2,256,128]{4,3,2,1,0:T(8,128)(2,1)}, bf16[2,4,2,256,128]{4,3,2,1,0:T(8,128)(2,1)S(1)}, u32[]{:S(2)}) copy-start(bf16[2,4,2,256,128]{4,3,2,1,0:T(8,128)(2,1)S(1)} %pad_maximum_fusion.5.refs_10_) | copy-start | bytes 3145732
  57.0 17.8 %copy-start.3 = (f32[1,2048,128]{2,1,0:T(8,128)S(1)}, f32[1,2048,128]{2,1,0:T(8,128)}, u32[]{:S(2)}) copy-start(f32[1,2048,128]{2,1,0:T(8,128)} %param.16) | copy-start | bytes 3145732
  57.0 36.9 %collective-permute-start.19 = (bf16[2,4,2,256,128]{4,3,2,1,0:T(8,128)(2,1)S(1)}, bf16[2,4,2,256,128]{4,3,2,1,0:T(8,128)(2,1)}, u32[]{:S(2)}, u32[]{:S(2)}) collective-permute-start(bf16[2,4,2,256,128]{4,3,2,1,0:T(8,128)(2,1)S(1)} %pad_maximum_fusion.5.refs_10_), channel_id=1, source_target_pairs={{0,8},{4,12},{8,0},{12,4},{16,24},{20,28},{24,16},{28,20},{1,9},{5... | collective-permute-start | bytes 3145736 | tf_op jit(solution)/shard_map/ppermute | solution.py:244
  68.3 27.3 %collective-permute-start.20 = (bf16[2,4,2,256,128]{4,3,2,1,0:T(8,128)(2,1)S(1)}, bf16[2,4,2,256,128]{4,3,2,1,0:T(8,128)(2,1)}, u32[]{:S(2)}, u32[]{:S(2)}) collective-permute-start(bf16[2,4,2,256,128]{4,3,2,1,0:T(8,128)(2,1)S(1)} %pad_maximum_fusion.5.refs_10_), channel_id=1, source_target_pairs={{0,16},{4,20},{8,24},{12,28},{16,0},{20,4},{24,8},{28,12},{1,17},{... | collective-permute-start | bytes 3145736 | tf_op jit(solution)/shard_map/ppermute | solution.py:244
  73.5 1.6 copy-start.4
  74.6 1.3 copy-start.5
  74.6 28.8 %collective-permute-start.7 = (bf16[2,4,2,256,128]{4,3,2,1,0:T(8,128)(2,1)}, bf16[2,4,2,256,128]{4,3,2,1,0:T(8,128)(2,1)}, u32[]{:S(2)}, u32[]{:S(2)}) collective-permute-start(bf16[2,4,2,256,128]{4,3,2,1,0:T(8,128)(2,1)} %pad_maximum_fusion.4.refs_0_), channel_id=1, source_target_pairs={{0,8},{4,12},{8,0},{12,4},{16,24},{20,28},{24,16},{28,20},{1,9},{5... | collective-permute-start | bytes 3145736 | tf_op jit(solution)/shard_map/ppermute | solution.py:244
  74.6 50.1 %collective-permute-start.8 = (bf16[2,4,2,256,128]{4,3,2,1,0:T(8,128)(2,1)}, bf16[2,4,2,256,128]{4,3,2,1,0:T(8,128)(2,1)}, u32[]{:S(2)}, u32[]{:S(2)}) collective-permute-start(bf16[2,4,2,256,128]{4,3,2,1,0:T(8,128)(2,1)} %pad_maximum_fusion.4.refs_0_), channel_id=1, source_target_pairs={{0,16},{4,20},{8,24},{12,28},{16,0},{20,4},{24,8},{28,12},{1,17},{... | collective-permute-start | bytes 3145736 | tf_op jit(solution)/shard_map/ppermute | solution.py:244
  79.3 14.0 %collective-permute-start.1 = (bf16[128,2048]{1,0:T(8,128)(2,1)}, bf16[128,2048]{1,0:T(8,128)(2,1)}, u32[]{:S(2)}, u32[]{:S(2)}) collective-permute-start(bf16[128,2048]{1,0:T(8,128)(2,1)} %param.11), channel_id=1, source_target_pairs={{0,1},{1,2},{2,3},{3,0},{4,7},{5,4},{6,5},{7,6},{8,9},{9,10},{10,1... | collective-permute-start | bytes 1572872 | tf_op jit(solution)/shard_map/ppermute | solution.py:262
  81.3 5.2 %copy-start.16 = (s32[6]{0:T(128)S(1)}, s32[6]{0:T(128)}, u32[]{:S(2)}) copy-start(s32[6]{0:T(128)} %param.21) | copy-start | bytes 76
  81.3 5.3 %copy-start.12 = (s32[6]{0:T(128)S(1)}, s32[6]{0:T(128)}, u32[]{:S(2)}) copy-start(s32[6]{0:T(128)} %param.19) | copy-start | bytes 76
  81.3 94.0 %all-to-all-start.1 = ((bf16[8,4,256,128]{3,2,1,0:T(8,128)(2,1)}), bf16[8,4,256,128]{3,2,1,0:T(8,128)(2,1)S(1)}, u32[]{:S(2)}, u32[]{:S(2)}) async-start(bf16[8,4,256,128]{3,2,1,0:T(8,128)(2,1)} %pad_maximum_fusion), calls=%async_computation.1 | async-start | bytes 4194304 | tf_op jit(solution)/shard_map/all_to_all | solution.py:436
  93.3 38.7 %collective-permute-start.21 = (bf16[2,4,2,256,128]{4,3,2,1,0:T(8,128)(2,1)S(1)}, bf16[2,4,2,256,128]{4,3,2,1,0:T(8,128)(2,1)S(1)}, u32[]{:S(2)}, u32[]{:S(2)}) collective-permute-start(bf16[2,4,2,256,128]{4,3,2,1,0:T(8,128)(2,1)S(1)} %pad_maximum_fusion.5.refs_10_), channel_id=1, source_target_pairs={{0,4},{4,0},{8,12},{12,8},{16,20},{20,16},{24,28},{28,24},{1,5},{5... | collective-permute-start | bytes 3145736 | tf_op jit(solution)/shard_map/ppermute | solution.py:244
  93.9 74.4 %collective-permute-start.9 = (bf16[2,4,2,256,128]{4,3,2,1,0:T(8,128)(2,1)}, bf16[2,4,2,256,128]{4,3,2,1,0:T(8,128)(2,1)}, u32[]{:S(2)}, u32[]{:S(2)}) collective-permute-start(bf16[2,4,2,256,128]{4,3,2,1,0:T(8,128)(2,1)} %pad_maximum_fusion.4.refs_0_), channel_id=1, source_target_pairs={{0,4},{4,0},{8,12},{12,8},{16,20},{20,16},{24,28},{28,24},{1,5},{5... | collective-permute-start | bytes 3145736 | tf_op jit(solution)/shard_map/ppermute | solution.py:244
  95.6 34.8 %collective-permute-start.2 = (bf16[128,2048]{1,0:T(8,128)(2,1)}, bf16[128,2048]{1,0:T(8,128)(2,1)S(1)}, u32[]{:S(2)}, u32[]{:S(2)}) collective-permute-start(bf16[128,2048]{1,0:T(8,128)(2,1)} %param.12), channel_id=1, source_target_pairs={{0,0},{1,1},{2,2},{3,3},{4,6},{5,7},{6,4},{7,5},{8,8},{9,9},{10,10... | collective-permute-start | bytes 1572872 | tf_op jit(solution)/shard_map/ppermute | solution.py:262
  103.4 27.0 %collective-permute-start.3 = (bf16[128,2048]{1,0:T(8,128)(2,1)}, bf16[128,2048]{1,0:T(8,128)(2,1)S(1)}, u32[]{:S(2)}, u32[]{:S(2)}) collective-permute-start(bf16[128,2048]{1,0:T(8,128)(2,1)} %param.12), channel_id=1, source_target_pairs={{0,1},{1,2},{2,3},{3,0},{4,7},{5,4},{6,5},{7,6},{8,9},{9,10},{10,1... | collective-permute-start | bytes 1572872 | tf_op jit(solution)/shard_map/ppermute | solution.py:262
  124.7 22.5 %collective-permute-start.24 = (bf16[4,2,256,128]{3,2,1,0:T(8,128)(2,1)S(1)}, bf16[4,2,256,128]{3,2,1,0:T(8,128)(2,1)}, u32[]{:S(2)}, u32[]{:S(2)}) collective-permute-start(bf16[4,2,256,128]{3,2,1,0:T(8,128)(2,1)S(1)} %slice_bitcast_fusion.1), channel_id=1, source_target_pairs={{0,16},{4,20},{8,24},{12,28},{16,0},{20,4},{24,8},{28,12},{1,17},{... | collective-permute-start | bytes 1572872 | tf_op jit(solution)/shard_map/ppermute | solution.py:244
  130.4 16.8 %copy-start.7 = (bf16[128,2048]{1,0:T(8,128)(2,1)}, bf16[128,2048]{1,0:T(8,128)(2,1)S(1)}, u32[]{:S(2)}) copy-start(bf16[128,2048]{1,0:T(8,128)(2,1)S(1)} %collective-permute-done.2) | copy-start | bytes 1572868
  130.4 42.8 %collective-permute-start.26 = (bf16[4,2,256,128]{3,2,1,0:T(8,128)(2,1)}, bf16[4,2,256,128]{3,2,1,0:T(8,128)(2,1)}, u32[]{:S(2)}, u32[]{:S(2)}) collective-permute-start(bf16[4,2,256,128]{3,2,1,0:T(8,128)(2,1)} %slice_bitcast_fusion), channel_id=1, source_target_pairs={{0,8},{4,12},{8,0},{12,4},{16,24},{20,28},{24,16},{28,20},{1,9},{5... | collective-permute-start | bytes 1572872 | tf_op jit(solution)/shard_map/ppermute | solution.py:244
  130.4 22.3 %copy-start.9 = (bf16[128,2048]{1,0:T(8,128)(2,1)}, bf16[128,2048]{1,0:T(8,128)(2,1)S(1)}, u32[]{:S(2)}) copy-start(bf16[128,2048]{1,0:T(8,128)(2,1)S(1)} %collective-permute-done.3) | copy-start | bytes 1572868
  130.4 43.3 %collective-permute-start.12 = (bf16[4,2,256,128]{3,2,1,0:T(8,128)(2,1)}, bf16[4,2,256,128]{3,2,1,0:T(8,128)(2,1)}, u32[]{:S(2)}, u32[]{:S(2)}) collective-permute-start(bf16[4,2,256,128]{3,2,1,0:T(8,128)(2,1)} %slice_bitcast_fusion.3), channel_id=1, source_target_pairs={{0,16},{4,20},{8,24},{12,28},{16,0},{20,4},{24,8},{28,12},{1,17},{... | collective-permute-start | bytes 1572872 | tf_op jit(solution)/shard_map/ppermute | solution.py:244
  131.9 20.9 %copy-start.13 = (bf16[2,4,2,256,128]{4,3,2,1,0:T(8,128)(2,1)}, bf16[2,4,2,256,128]{4,3,2,1,0:T(8,128)(2,1)S(1)}, u32[]{:S(2)}) copy-start(bf16[2,4,2,256,128]{4,3,2,1,0:T(8,128)(2,1)S(1)} %collective-permute-done.21.refs_13_) | copy-start | bytes 3145732
  131.9 41.8 %collective-permute-start.14 = (bf16[4,2,256,128]{3,2,1,0:T(8,128)(2,1)}, bf16[4,2,256,128]{3,2,1,0:T(8,128)(2,1)}, u32[]{:S(2)}, u32[]{:S(2)}) collective-permute-start(bf16[4,2,256,128]{3,2,1,0:T(8,128)(2,1)} %slice_bitcast_fusion.2), channel_id=1, source_target_pairs={{0,8},{4,12},{8,0},{12,4},{16,24},{20,28},{24,16},{28,20},{1,9},{5... | collective-permute-start | bytes 1572872 | tf_op jit(solution)/shard_map/ppermute | solution.py:244
  147.2 27.0 %collective-permute-start.25 = (bf16[4,2,256,128]{3,2,1,0:T(8,128)(2,1)}, bf16[4,2,256,128]{3,2,1,0:T(8,128)(2,1)}, u32[]{:S(2)}, u32[]{:S(2)}) collective-permute-start(bf16[4,2,256,128]{3,2,1,0:T(8,128)(2,1)} %collective-permute-done.24.refs_16_), channel_id=1, source_target_pairs={{0,4},{4,0},{8,12},{12,8},{16,20},{20,16},{24,28},{28,24},{1,5},{5... | collective-permute-start | bytes 1572872 | tf_op jit(solution)/shard_map/ppermute | solution.py:244
  152.7 21.6 %copy-start.8 = (bf16[128,2048]{1,0:T(8,128)(2,1)S(1)}, bf16[128,2048]{1,0:T(8,128)(2,1)}, u32[]{:S(2)}) copy-start(bf16[128,2048]{1,0:T(8,128)(2,1)} %copy-done.7) | copy-start | bytes 1572868
  152.8 21.4 %copy-start.10 = (bf16[128,2048]{1,0:T(8,128)(2,1)S(1)}, bf16[128,2048]{1,0:T(8,128)(2,1)}, u32[]{:S(2)}) copy-start(bf16[128,2048]{1,0:T(8,128)(2,1)} %copy-done.9) | copy-start | bytes 1572868
  168.3 12.1 %collective-permute-start.22 = (bf16[2,4,2,256,128]{4,3,2,1,0:T(8,128)(2,1)}, bf16[2,4,2,256,128]{4,3,2,1,0:T(8,128)(2,1)}, u32[]{:S(2)}, u32[]{:S(2)}) collective-permute-start(bf16[2,4,2,256,128]{4,3,2,1,0:T(8,128)(2,1)} %collective-permute-done.19.refs_11_), channel_id=1, source_target_pairs={{0,4},{4,0},{8,12},{12,8},{16,20},{20,16},{24,28},{28,24},{1,5},{5... | collective-permute-start | bytes 3145736 | tf_op jit(solution)/shard_map/ppermute | solution.py:244
  173.2 14.8 %collective-permute-start.23 = (bf16[2,4,2,256,128]{4,3,2,1,0:T(8,128)(2,1)}, bf16[2,4,2,256,128]{4,3,2,1,0:T(8,128)(2,1)}, u32[]{:S(2)}, u32[]{:S(2)}) collective-permute-start(bf16[2,4,2,256,128]{4,3,2,1,0:T(8,128)(2,1)} %collective-permute-done.20.refs_12_), channel_id=1, source_target_pairs={{0,4},{4,0},{8,12},{12,8},{16,20},{20,16},{24,28},{28,24},{1,5},{5... | collective-permute-start | bytes 3145736 | tf_op jit(solution)/shard_map/ppermute | solution.py:244
  173.7 14.3 %collective-permute-start.10 = (bf16[2,4,2,256,128]{4,3,2,1,0:T(8,128)(2,1)}, bf16[2,4,2,256,128]{4,3,2,1,0:T(8,128)(2,1)}, u32[]{:S(2)}, u32[]{:S(2)}) collective-permute-start(bf16[2,4,2,256,128]{4,3,2,1,0:T(8,128)(2,1)} %collective-permute-done.7.refs_1_), channel_id=1, source_target_pairs={{0,4},{4,0},{8,12},{12,8},{16,20},{20,16},{24,28},{28,24},{1,5},{5... | collective-permute-start | bytes 3145736 | tf_op jit(solution)/shard_map/ppermute | solution.py:244
  173.8 14.3 %collective-permute-start.11 = (bf16[2,4,2,256,128]{4,3,2,1,0:T(8,128)(2,1)}, bf16[2,4,2,256,128]{4,3,2,1,0:T(8,128)(2,1)}, u32[]{:S(2)}, u32[]{:S(2)}) collective-permute-start(bf16[2,4,2,256,128]{4,3,2,1,0:T(8,128)(2,1)} %collective-permute-done.8.refs_2_), channel_id=1, source_target_pairs={{0,4},{4,0},{8,12},{12,8},{16,20},{20,16},{24,28},{28,24},{1,5},{5... | collective-permute-start | bytes 3145736 | tf_op jit(solution)/shard_map/ppermute | solution.py:244
  174.2 5.9 %collective-permute-start.27 = (bf16[4,2,256,128]{3,2,1,0:T(8,128)(2,1)}, bf16[4,2,256,128]{3,2,1,0:T(8,128)(2,1)}, u32[]{:S(2)}, u32[]{:S(2)}) collective-permute-start(bf16[4,2,256,128]{3,2,1,0:T(8,128)(2,1)} %collective-permute-done.26.refs_18_), channel_id=1, source_target_pairs={{0,4},{4,0},{8,12},{12,8},{16,20},{20,16},{24,28},{28,24},{1,5},{5... | collective-permute-start | bytes 1572872 | tf_op jit(solution)/shard_map/ppermute | solution.py:244
  180.1 7.9 %collective-permute-start.13 = (bf16[4,2,256,128]{3,2,1,0:T(8,128)(2,1)}, bf16[4,2,256,128]{3,2,1,0:T(8,128)(2,1)S(1)}, u32[]{:S(2)}, u32[]{:S(2)}) collective-permute-start(bf16[4,2,256,128]{3,2,1,0:T(8,128)(2,1)} %collective-permute-done.12.refs_6_), channel_id=1, source_target_pairs={{0,4},{4,0},{8,12},{12,8},{16,20},{20,16},{24,28},{28,24},{1,5},{5... | collective-permute-start | bytes 1572872 | tf_op jit(solution)/shard_map/ppermute | solution.py:244
  180.4 7.6 %collective-permute-start.15 = (bf16[4,2,256,128]{3,2,1,0:T(8,128)(2,1)}, bf16[4,2,256,128]{3,2,1,0:T(8,128)(2,1)S(1)}, u32[]{:S(2)}, u32[]{:S(2)}) collective-permute-start(bf16[4,2,256,128]{3,2,1,0:T(8,128)(2,1)} %collective-permute-done.14.refs_8_), channel_id=1, source_target_pairs={{0,4},{4,0},{8,12},{12,8},{16,20},{20,16},{24,28},{28,24},{1,5},{5... | collective-permute-start | bytes 1572872 | tf_op jit(solution)/shard_map/ppermute | solution.py:244
  184.2 39.9 %all-to-all-start.2 = ((bf16[8,4,256,128]{3,2,1,0:T(8,128)(2,1)}), bf16[8,4,256,128]{3,2,1,0:T(8,128)(2,1)S(1)}, u32[]{:S(2)}, u32[]{:S(2)}) async-start(bf16[8,4,256,128]{3,2,1,0:T(8,128)(2,1)} %dynamic-slice_dynamic-update-slice_fusion), calls=%async_computation.2 | async-start | bytes 4194304 | tf_op jit(solution)/shard_map/all_to_all | solution.py:438
  188.0 0.9 copy-start.15
  222.5 2.9 %collective-permute-start.28 = (bf16[2,2048,128]{2,1,0:T(8,128)(2,1)}, bf16[2,2048,128]{2,1,0:T(8,128)(2,1)S(1)}, u32[]{:S(2)}, u32[]{:S(2)}) collective-permute-start(bf16[2,2048,128]{2,1,0:T(8,128)(2,1)} %fusion.2), channel_id=1, source_target_pairs={{0,4},{4,0},{8,12},{12,8},{16,20},{20,16},{24,28},{28,24},{1,5},{5... | collective-permute-start | bytes 3145736 | tf_op jit(solution)/shard_map/ppermute | solution.py:244
  224.6 2.2 copy-start
  225.2 2.0 copy-start.1
  (1 other events, 0.8 us)
